TPU v7x, 32 devices: a whole 2x2x4 slice. The times are simulated.
32 devices in a mesh: cohort: 2 (over x), tile: 16 (over z, y, core).
Axes of the slice: x: 2, y: 2, z: 4, core: 2. Of those that a mesh axis runs over, the one named last changes fastest.
Arguments:
- dosage: bfloat16 [512, 8192], P(('cohort', 'tile')), parts along dimension 0, may hold values from 0 to 2
- covars: float32 [512, 16], P(('cohort', 'tile')), parts along dimension 0, may hold values from -12 to 12, as said below
- phenotypes: float32 [512, 1792], P(('cohort', 'tile')), parts along dimension 0, may hold values from -100 to 100
Outputs:
- mean_chi: float32 [3584], P(('cohort', 'tile')), parts along dimension 0
- hit_rate: float32 [3584], P(('cohort', 'tile')), parts along dimension 0
There are 2 independent parts, one for each index of `cohort`. A program takes and returns all parts, laid end to end along the dimension named above; each array names one. Nothing has to cross between parts.
Inputs may be any that keep to these rules, and one draw needn't show every extreme that they name: `covars`: each covariate column has its own mean and spread.
All inputs are finite; a program needn't handle non-finite values.
Results may differ from a plain program's by a relative error of at most 0.003.
Values may be sent and summed in bfloat16 or wider, within the bound.
A program may use at most 64 MiB of HBM per device.

v0:
```python
import functools

import jax
import jax.numpy as jnp
from jax import lax
from jax.experimental import pallas as pl
from jax.experimental.pallas import tpu as pltpu
from jax.sharding import PartitionSpec as P

LANES = 128
HIGH = lax.Precision.HIGHEST


def dot(a, b, ca, cb, precision=HIGH):
    return lax.dot_general(
        a, b, (((ca,), (cb,)), ((), ())), precision=precision, preferred_element_type=jnp.float32
    )


def inverse(gram):
    size = gram.shape[0]
    row_id = lax.broadcasted_iota(jnp.int32, (size, 2 * size), 0)
    eye = (
        lax.broadcasted_iota(jnp.int32, (size, size), 0)
        == lax.broadcasted_iota(jnp.int32, (size, size), 1)
    ).astype(jnp.float32)
    work = jnp.concatenate([gram, eye], axis=1)
    for k in range(size):
        row = work[k : k + 1, :] / work[k : k + 1, k : k + 1]
        work = jnp.where(row_id == k, row, work - work[:, k : k + 1] * row)
    return work[:, size:]


def partner(a, k, count):
    if count & (count - 1):
        return lax.rem(a + k, count)
    out, bit = 0, 1
    while bit < count:
        out = out + lax.rem(a // bit + k // bit, 2) * bit
        bit *= 2
    return out


def kernel(
    n, zs, ys, cs, own,
    dose_in, cov_in, pheno_in, out_ref,
    dose_ref, cov_ref, pheno_ref, load_sem,
    cov_all, raw, dose_all, blocks, doset, scale, part, landed,
    cov_own, cov_send, cov_recv, raw_send, raw_recv, dose_send, dose_recv,
    z_send, pass_send, c_send, blk_recv, part_send, part_recv,
):
    me = lax.axis_index("tile")
    rows, variants = dose_ref.shape
    covs = cov_ref.shape[1]
    genes = pheno_ref.shape[1]
    nb = genes // (ys * LANES)
    peers = zs * cs
    width = variants // peers
    samples = rows * n
    c = lax.rem(me, cs)
    y = lax.rem(me // cs, ys)
    z = me // (cs * ys)
    place = z * cs + c

    def index(zi, yi, ci):
        return (zi * ys + yi) * cs + ci

    def place_of(t):
        return t // (cs * ys) * cs + lax.rem(t, cs)

    def at_place(p):
        return index(p // cs, y, lax.rem(p, cs))

    def remote(src, dst, ssem, rsem, dev):
        return pltpu.make_async_remote_copy(
            src_ref=src, dst_ref=dst, send_sem=ssem, recv_sem=rsem,
            device_id={"tile": dev}, device_id_type=pl.DeviceIdType.MESH,
        )

    def row_slice(t):
        return pl.ds(pl.multiple_of(t * rows, rows), rows)

    def lane_slice(start, size):
        return pl.ds(pl.multiple_of(start, LANES), size)

    cov_load = pltpu.make_async_copy(cov_in, cov_ref, load_sem.at[0])
    pheno_load = pltpu.make_async_copy(pheno_in, pheno_ref, load_sem.at[1])
    dose_load = pltpu.make_async_copy(dose_in, dose_ref, load_sem.at[2])
    barrier = pltpu.get_barrier_semaphore()
    for k in range(1, n):
        pl.semaphore_signal(
            barrier, inc=1, device_id={"tile": lax.rem(me + k, n)},
            device_id_type=pl.DeviceIdType.MESH,
        )
    cov_load.start()
    pheno_load.start()
    dose_load.start()
    cov_load.wait()
    groups = rows // 8
    packed = [cov_ref[8 * g : 8 * g + 8, :] for g in range(groups)]
    fill = jnp.zeros((8, LANES - groups * covs), jnp.float32)
    cov_own[...] = jnp.concatenate(packed + [fill], axis=1)
    pheno_load.wait()
    dose_load.wait()
    pl.semaphore_wait(barrier, n - 1)

    def cov_copy(src, dev):
        return remote(cov_own, cov_all.at[src], cov_send.at[dev], cov_recv.at[src], dev)

    def raw_copy(src, dev):
        return remote(
            pheno_ref.at[:, lane_slice((lax.rem(dev // cs, ys) * nb + place_of(dev)) * LANES, LANES)],
            raw.at[row_slice(src), :], raw_send.at[dev], raw_recv.at[src], dev,
        )

    def dose_copy(src, dev):
        return remote(
            dose_ref.at[:, lane_slice(place_of(dev) * width, width)],
            dose_all.at[row_slice(src), :], dose_send.at[dev], dose_recv.at[src], dev,
        )

    def others(body):
        @pl.loop(1, n)
        def _(k):
            body(partner(me, k, n))

    others(lambda dev: cov_copy(me, dev).start())

    def send_first(dev):
        @pl.when(place_of(dev) < nb)
        def _():
            raw_copy(me, dev).start()

    def group(body):
        @pl.loop(1, peers)
        def _(k):
            body(at_place(partner(place, k, peers)))

    y_dev = index(z, lax.rem(y + 1, ys), c)
    c_dev = index(z, y, lax.rem(c + 1, cs))

    def dose_pass(src):
        return remote(
            dose_all.at[row_slice(src), :], dose_all.at[row_slice(src), :],
            pass_send.at[src], dose_recv.at[src], y_dev,
        )

    others(send_first)
    group(lambda dev: dose_copy(me, dev).start())
    if ys > 1:
        dose_copy(me, y_dev).start()

    cov_all[me] = cov_own[...]
    dose_all[row_slice(me), :] = dose_ref[:, lane_slice(place * width, width)]

    others(lambda src: cov_copy(src, me).wait_recv())
    tiles = cov_all[...]
    cov = jnp.concatenate(
        [tiles[:, :, g * covs : (g + 1) * covs] for g in range(groups)], axis=1
    ).reshape(samples, covs)
    eye = (
        lax.broadcasted_iota(jnp.int32, (covs, covs), 0)
        == lax.broadcasted_iota(jnp.int32, (covs, covs), 1)
    ).astype(jnp.float32)
    covt = dot(eye, cov, 1, 1)
    solve = dot(cov, inverse(dot(covt, cov, 1, 0)), 1, 0)
    solve_parts = jnp.concatenate([solve] * 3, axis=1)
    cov_hi = cov.astype(jnp.bfloat16)
    cov_rest = cov - cov_hi.astype(jnp.float32)
    cov_mid = cov_rest.astype(jnp.bfloat16)
    cov_low = cov_rest - cov_mid.astype(jnp.float32)
    cov_parts = jnp.concatenate(
        [cov_hi.astype(jnp.float32), cov_mid.astype(jnp.float32), cov_low], axis=1
    ).astype(jnp.bfloat16)

    def blk_z(o, dev):
        return remote(blocks.at[o], blocks.at[o], z_send.at[dev // (cs * ys)], blk_recv.at[o], dev)

    def blk_c(o, dev):
        return remote(blocks.at[o], blocks.at[o], c_send.at[o], blk_recv.at[o], dev)

    @pl.when(place < nb)
    def _():
        raw[row_slice(me), :] = pheno_ref[:, lane_slice((y * nb + place) * LANES, LANES)]
        others(lambda src: raw_copy(src, me).wait_recv())
        pheno = raw[...]
        resid = pheno - dot(solve, dot(covt, pheno, 1, 0), 1, 0)
        var = jnp.sum(resid * resid, axis=0, keepdims=True) / samples + 0.1
        inv = 1.0 / var
        hi = inv.astype(jnp.bfloat16)
        rest = inv - hi.astype(jnp.float32)
        mid = rest.astype(jnp.bfloat16)
        low = (rest - mid.astype(jnp.float32)).astype(jnp.bfloat16)
        line = lax.broadcasted_iota(jnp.int32, (16, LANES), 0)
        extra = jnp.where(
            line == 0, hi.astype(jnp.float32),
            jnp.where(line == 1, mid.astype(jnp.float32),
                      jnp.where(line == 2, low.astype(jnp.float32), 0.0)),
        )
        blocks[place, pl.ds(samples, 16), :] = extra.astype(jnp.bfloat16)
        blocks[place, pl.ds(0, samples), :] = resid.astype(jnp.bfloat16)
        for k in range(1, zs):
            blk_z(place, index(partner(z, k, zs), y, c)).start()
        if cs > 1:
            blk_c(place, c_dev).start()

    def hand_on(src):
        dose_copy(src, me).wait_recv()
        if ys > 1:
            dose_pass(src).start()

    group(hand_on)
    if ys > 1:
        @pl.loop(0, peers)
        def _(k):
            p = partner(place, k, peers)
            src = index(p // cs, lax.rem(y + 1, ys), lax.rem(p, cs))
            dose_copy(src, me).wait_recv()

    dose_bf = dose_all[...].T
    cov_dose = dot(dose_bf, cov_parts, 1, 0, None)
    dose = dose_bf.astype(jnp.float32) - dot(cov_dose, solve_parts, 1, 1)
    doset[...] = dose.astype(jnp.bfloat16)
    dose_var = jnp.sum(dose * dose, axis=1, keepdims=True) / samples + 0.1
    scale[...] = jnp.broadcast_to(1.0 / (samples * dose_var), scale.shape)

    def compute(o):
        extra = blocks[o, pl.ds(samples, 16), :].astype(jnp.float32)
        gene_scale = jnp.sum(extra[0:3, :], axis=0, keepdims=True)
        cross = dot(doset[...], blocks[o, pl.ds(0, samples), :], 1, 0, None)
        chi = cross * cross * (scale[...] * gene_scale)
        hit = 1.0 / (1.0 + jnp.exp(-2.0 * (chi - 4.0)))
        cols = lane_slice(o * LANES, LANES)
        part[0:1, cols] = jnp.sum(chi, axis=0, keepdims=True)
        part[1:2, cols] = jnp.sum(hit, axis=0, keepdims=True)

    @pl.when(place < nb)
    def _():
        compute(place)

    @pl.loop(1, zs)
    def _(k):
        o = partner(z, k, zs) * cs + c

        @pl.when(o < nb)
        def _():
            blk_z(o, me).wait_recv()
            if cs > 1:
                blk_c(o, c_dev).start()
            compute(o)

    if cs > 1:
        @pl.loop(0, zs)
        def _(k):
            o = partner(z, k, zs) * cs + lax.rem(c + 1, cs)

            @pl.when(o < nb)
            def _():
                blk_c(o, me).wait_recv()
                compute(o)

    window = landed.shape[2]

    def owner(k):
        return y * peers + partner(place, k, peers)

    def first(dev):
        return jnp.minimum(own * lax.rem(dev, peers) // LANES * LANES, nb * LANES - window)

    def part_copy(src, dev):
        return remote(
            part.at[:, lane_slice(first(dev), window)], landed.at[place_of(src)],
            part_send.at[lax.rem(dev, peers)], part_recv.at[place_of(src)], dev,
        )

    def each_part(body):
        @pl.loop(0, peers)
        def _(k):
            dev = owner(k)

            @pl.when(dev != me)
            def _():
                body(dev)

    def each_source(body):
        @pl.loop(0, peers)
        def _(k):
            src = index(k // cs, me // peers, lax.rem(k, cs))

            @pl.when(src != me)
            def _():
                body(src)

    each_part(lambda dev: part_copy(me, dev).start())

    @pl.when(me // peers == y)
    def _():
        landed[place] = part[:, lane_slice(first(me), window)]

    each_source(lambda src: part_copy(src, me).wait_recv())
    total = jnp.sum(landed[...], axis=0)
    shift = own * lax.rem(me, peers) - first(me)
    out_ref[...] = pltpu.roll(total, lax.rem(window - shift, window), 1)

    def drain(dev):
        cov_copy(me, dev).wait_send()

        @pl.when(place_of(dev) < nb)
        def _():
            raw_copy(me, dev).wait_send()

    others(drain)

    def drain_dose(dev):
        dose_copy(me, dev).wait_send()
        if ys > 1:
            dose_pass(dev).wait_send()

    group(drain_dose)
    if ys > 1:
        dose_copy(me, y_dev).wait_send()
    each_part(lambda dev: part_copy(me, dev).wait_send())

    @pl.when(place < nb)
    def _():
        for k in range(1, zs):
            blk_z(place, index(partner(z, k, zs), y, c)).wait_send()

    if cs > 1:
        @pl.loop(0, zs)
        def _(k):
            o = partner(z, k, zs) * cs + c

            @pl.when(o < nb)
            def _():
                blk_c(o, c_dev).wait_send()


def local(dosage, covars, phenotypes):
    n = lax.axis_size("tile")
    rows, variants = dosage.shape
    genes = phenotypes.shape[1]
    covs = covars.shape[1]
    samples = rows * n
    cs = 2 if n % 2 == 0 else 1
    ys = 2 if n % (2 * cs) == 0 else 1
    zs = n // (cs * ys)
    peers = zs * cs
    nb = genes // (ys * LANES)
    own = genes // n
    width = variants // peers
    window = (own + LANES - 1 + LANES - 1) // LANES * LANES
    dma = pltpu.SemaphoreType.DMA
    out = pl.pallas_call(
        functools.partial(kernel, n, zs, ys, cs, own),
        out_shape=jax.ShapeDtypeStruct((2, window), jnp.float32),
        in_specs=[pl.BlockSpec(memory_space=pl.ANY)] * 3,
        out_specs=pl.BlockSpec(memory_space=pltpu.VMEM),
        scratch_shapes=[
            pltpu.VMEM(dosage.shape, dosage.dtype),
            pltpu.VMEM(covars.shape, covars.dtype),
            pltpu.VMEM(phenotypes.shape, phenotypes.dtype),
            dma((3,)),
            pltpu.VMEM((n, 8, LANES), jnp.float32),
            pltpu.VMEM((samples, LANES), jnp.float32),
            pltpu.VMEM((samples, width), jnp.bfloat16),
            pltpu.VMEM((nb, samples + 16, LANES), jnp.bfloat16),
            pltpu.VMEM((width, samples), jnp.bfloat16),
            pltpu.VMEM((width, LANES), jnp.float32),
            pltpu.VMEM((2, nb * LANES), jnp.float32),
            pltpu.VMEM((peers, 2, window), jnp.float32),
            pltpu.VMEM((8, LANES), jnp.float32),
            dma((n,)), dma((n,)), dma((n,)), dma((n,)), dma((n,)), dma((n,)),
            dma((zs,)), dma((n,)), dma((nb,)), dma((nb,)), dma((peers,)), dma((peers,)),
        ],
        compiler_params=pltpu.CompilerParams(collective_id=0, has_side_effects=True),
    )(dosage, covars, phenotypes)
    return out[0, :own] / variants, 20.0 / variants * out[1, :own]


def solution(mesh):
    spec = P(("cohort", "tile"), None)
    return jax.shard_map(
        local,
        mesh=mesh,
        in_specs=(spec, spec, spec),
        out_specs=(P(("cohort", "tile")), P(("cohort", "tile"))),
        check_vma=False,
    )
```

profile of v0, /device:TPU:0, one launch (start us, length us, event | category | flops | bytes accessed | tf_op | source)
XLA Modules:
  0.0 33.2 jit_solution(5995702155786302975)
XLA Ops:
  0.6 31.3 %shard_map.50 = f32[2,256]{1,0:T(2,128)} custom-call(bf16[16,8192]{1,0:T(8,128)(2,1)} %dose_in.1, f32[16,16]{1,0:T(8,128)} %cov_in.1, f32[16,1792]{1,0:T(8,128)} %pheno_in.1), custom_call_target="tpu_custom_call" | custom-call | tf_op jit(solution)/shard_map/pallas_call | solution.py:354
  31.9 1.3 %multiply_bitcast_fusion = (f32[112]{0:T(128)}, f32[112]{0:T(128)}) fusion(f32[2,256]{1,0:T(2,128)} %shard_map.50), kind=kLoop, calls=%fused_computation | loop fusion | flops 224 | bytes 1792 | tf_op jit(solution)/shard_map/mul | solution.py:378
where the time goes:
time: 33.4 us; the launch traced here: 33.2 us
  Pallas kernels  31.3 us (94%)
  other arithmetic  1.25 us (4%)
  between operations  0.64 us (2%)
    pallas_call x1, Pallas kernels, local(): pl.pallas_call(functools.partial(kernel, n, zs, ys, cs, own), out_shape=j...  31.3 us
    mul x1, other arithmetic, local(): return (out[0, :own] / variants, 20.0 / variants * out[1, :own])  1.25 us

commit v1 on v0

v1 whole, which is shorter than its diff:
```python
import functools

import jax
import jax.numpy as jnp
from jax import lax
from jax.experimental import pallas as pl
from jax.experimental.pallas import tpu as pltpu
from jax.sharding import PartitionSpec as P

LANES = 128
CHUNK = 256
HIGH = lax.Precision.HIGHEST
F32 = jnp.float32
BF16 = jnp.bfloat16


def dot(a, b, ca, cb, precision=None):
    return lax.dot_general(
        a, b, (((ca,), (cb,)), ((), ())), precision=precision, preferred_element_type=F32
    )


def split(a, parts):
    out = []
    for _ in range(parts):
        term = a.astype(BF16)
        out.append(term)
        a = a - term.astype(F32)
    return out


def inverse_factor(gram):
    size = gram.shape[0]
    wide = 2 * size
    row_id = lax.broadcasted_iota(jnp.int32, (size, wide), 0)
    eye = (
        lax.broadcasted_iota(jnp.int32, (size, size), 0)
        == lax.broadcasted_iota(jnp.int32, (size, size), 1)
    ).astype(F32)
    work = jnp.concatenate([gram, eye], axis=1)
    for k in range(0, size, 2):
        one = jnp.broadcast_to(work[:, k : k + 1], (size, wide))
        two = jnp.broadcast_to(work[:, k + 1 : k + 2], (size, wide))
        first = lax.rsqrt(one[k : k + 1, :])
        below = two[k : k + 1, :] * first
        second = lax.rsqrt(two[k + 1 : k + 2, :] - below * below)
        top = work[k : k + 1, :] * first
        low = (work[k + 1 : k + 2, :] - below * top) * second
        left = one * first
        right = (two - left * below) * second
        rest = work - left * top - right * low
        work = jnp.where(
            row_id > k + 1, rest, jnp.where(row_id == k, top, jnp.where(row_id == k + 1, low, work))
        )
    return work[:, size:]


def kernel(
    n, zs, ys, cs, own, group,
    dose_in, cov_in, pheno_in, out_ref,
    dose_ref, pheno_ref, load_sem, cov_all, raw, dose_all, pt, acc, part, landed,
    cov_send, cov_recv, b_send, b_recv, zr_send, zl_send, z_recv, c_send, c_recv,
    d_send, dy_send, d_recv, pass_send, p_recv, part_send, part_recv,
):
    me = lax.axis_index("tile")
    rows, variants = dose_in.shape
    covs = cov_in.shape[1]
    samples = rows * n
    gh = raw.shape[-1]
    width = dose_all.shape[-1]
    peers = n // ys
    c = lax.rem(me, cs)
    y = lax.rem(me // cs, ys)
    z = me // (cs * ys)
    oc = lax.rem(c + 1, cs)
    oy = lax.rem(y + 1, ys)
    place = z * cs + c

    def index(zi, yi, ci):
        return (zi * ys + yi) * cs + ci

    def remote(src, dst, ssem, rsem, dev):
        return pltpu.make_async_remote_copy(
            src_ref=src, dst_ref=dst, send_sem=ssem, recv_sem=rsem,
            device_id={"tile": dev}, device_id_type=pl.DeviceIdType.MESH,
        )

    def lane_slice(start, size):
        return pl.ds(pl.multiple_of(start, LANES), size)

    def peer(k):
        return lax.rem(me + k, n)

    loads = [
        pltpu.make_async_copy(cov_in, cov_all.at[z, c, y], load_sem.at[0]),
        pltpu.make_async_copy(
            pheno_in.at[:, lane_slice(y * gh, gh)], raw.at[z, c, y], load_sem.at[1]
        ),
        pltpu.make_async_copy(
            pheno_in.at[:, lane_slice(oy * gh, gh)], pheno_ref, load_sem.at[2]
        ),
        pltpu.make_async_copy(dose_in, dose_ref, load_sem.at[3]),
        pltpu.make_async_copy(
            dose_in.at[:, lane_slice(place * width, width)], dose_all.at[z, c, y], load_sem.at[4]
        ),
    ]
    for load in loads:
        load.start()
    barrier = pltpu.get_barrier_semaphore()
    for k in range(1, n):
        pl.semaphore_signal(
            barrier, inc=1, device_id={"tile": peer(k)}, device_id_type=pl.DeviceIdType.MESH
        )
    for load in loads:
        load.wait()
    pl.semaphore_wait(barrier, n - 1)

    def cov_copy(k):
        own_cov = cov_all.at[z, c, y]
        return remote(own_cov, own_cov, cov_send.at[k], cov_recv.at[k], peer(k))

    def cov_wait(k):
        src = lax.rem(me + n - k, n)
        slot = cov_all.at[src // (cs * ys), lax.rem(src, cs), lax.rem(src // cs, ys)]
        return remote(slot, slot, cov_send.at[k], cov_recv.at[k], src)

    for k in range(1, n):
        cov_copy(k).start()

    def across():
        return remote(pheno_ref, raw.at[z, c, y], b_send, b_recv, index(z, oy, c))

    def slot_of(p, d):
        return raw.at[p, c, lax.rem(y + d, ys)]

    def to_right(p, d):
        slot = slot_of(p, d)
        return remote(slot, slot, zr_send.at[p, d], z_recv.at[p, d], index(z + 1, y, c))

    def to_left(p, d):
        slot = slot_of(p, d)
        return remote(slot, slot, zl_send.at[p, d], z_recv.at[p, d], index(z - 1, y, c))

    def to_core(p, d):
        slot = slot_of(p, d)
        return remote(slot, slot, c_send.at[p, d], c_recv.at[p], index(z, y, oc))

    def from_core(p):
        slot = raw.at[p, oc]
        return remote(slot, slot, c_send.at[p, 0], c_recv.at[p], index(z, y, oc))

    def spread(d):
        @pl.when(z + 1 < zs)
        def _():
            to_right(z, d).start()

        @pl.when(z > 0)
        def _():
            to_left(z, d).start()

        if cs > 1:
            to_core(z, d).start()

    def dose_copy(p, ci):
        return remote(
            dose_ref.at[:, lane_slice((p * cs + ci) * width, width)], dose_all.at[z, c, y],
            d_send.at[p, ci], d_recv.at[z], index(p, y, ci),
        )

    def dose_across(ci):
        return remote(
            dose_ref.at[:, lane_slice((z * cs + ci) * width, width)], dose_all.at[z, c, y],
            dy_send.at[ci], p_recv.at[z], index(z, oy, ci),
        )

    def dose_pass(p):
        slot = dose_all.at[p, :, y]
        return remote(slot, slot, pass_send.at[p], p_recv.at[p], index(z, oy, c))

    def dose_wait(p):
        slot = dose_all.at[p, :, y]
        return remote(slot, slot, pass_send.at[p], d_recv.at[p], me)

    def across_wait(p):
        slot = dose_all.at[p, :, oy]
        return remote(slot, slot, pass_send.at[p], p_recv.at[p], me)

    def each_side(k, body):
        @pl.when(z >= k)
        def _():
            body(z - k)

        @pl.when(z + k < zs)
        def _():
            body(z + k)

    def send_doses(p):
        for ci in range(cs):
            dose_copy(p, ci).start()

    if ys > 1:
        across().start()
    spread(0)
    if cs > 1:
        dose_copy(z, oc).start()
    if ys > 1:
        for ci in range(cs):
            dose_across(ci).start()
    each_side(1, send_doses)
    if ys > 1:
        remote(pheno_ref, raw.at[z, c, oy], b_send, b_recv, index(z, oy, c)).wait_recv()
        spread(1)
    for k in range(2, zs):
        each_side(k, send_doses)

    def relay(k):
        for d in range(ys):
            @pl.when(z >= k)
            def _():
                p = z - k
                to_right(p, d).wait_recv()

                @pl.when(z + 1 < zs)
                def _():
                    to_right(p, d).start()

                if cs > 1:
                    to_core(p, d).start()

            @pl.when(z + k < zs)
            def _():
                p = z + k
                to_left(p, d).wait_recv()

                @pl.when(z > 0)
                def _():
                    to_left(p, d).start()

                if cs > 1:
                    to_core(p, d).start()

    def hand_on(p):
        dose_wait(p).wait_recv()
        if ys > 1:
            dose_pass(p).start()

    for k in range(1, zs):
        relay(k)
        each_side(k, hand_on)
    if cs > 1:
        slot = dose_all.at[z, oc, y]
        remote(slot, slot, d_send.at[z, oc], d_recv.at[z], me).wait_recv()

    for k in range(1, n):
        cov_wait(k).wait_recv()
    cov = cov_all[...].reshape(samples, covs)
    covt = cov.T
    factor = inverse_factor(dot(covt, cov, 1, 0, HIGH))
    basist = dot(factor, covt, 1, 0, HIGH)
    eye = (
        lax.broadcasted_iota(jnp.int32, (covs, covs), 0)
        == lax.broadcasted_iota(jnp.int32, (covs, covs), 1)
    ).astype(F32)
    fix = 1.5 * eye - 0.5 * dot(basist, basist, 1, 1, HIGH)
    basist = dot(fix, basist, 1, 0, HIGH)
    bt_hi, bt_mid, bt_low = [t.astype(F32) for t in split(basist, 3)]
    bt = jnp.concatenate([bt_hi, bt_mid, bt_low], axis=0).astype(BF16)
    b_hi, b_mid, b_low = [t.astype(F32) for t in split(basist.T, 3)]
    basis = jnp.concatenate([b_hi, b_hi, b_hi, b_mid, b_mid, b_low], axis=1).astype(BF16)

    if cs > 1:
        for p in range(zs):
            from_core(p).wait_recv()

    def residual(at):
        cols = lane_slice(at, LANES)
        pheno = raw[:, :, :, :, cols].reshape(samples, LANES)
        hi, mid, low = split(pheno, 3)
        with_hi = dot(bt, hi, 1, 0)
        with_mid = dot(bt[0 : 2 * covs], mid, 1, 0)
        coef = (
            with_hi[0:covs]
            + (with_hi[covs : 2 * covs] + with_mid[0:covs])
            + (with_hi[2 * covs :] + with_mid[covs:] + dot(bt[0:covs], low, 1, 0))
        )
        one, two, three = [t.astype(F32) for t in split(coef, 3)]
        stack = jnp.concatenate([one, two, three, one, two, one], axis=0).astype(BF16)
        resid = pheno - dot(basis, stack, 1, 0)
        var = jnp.sum(resid * resid, axis=0, keepdims=True) / samples + 0.1
        resid = (resid * lax.rsqrt(var)).T
        hi, low = split(resid, 2)
        genes_at = pl.ds(pl.multiple_of(at, LANES), LANES)
        pt[genes_at, 0:samples] = hi
        pt[genes_at, samples:] = low

    @pl.loop(0, gh // (group * LANES))
    def _(b):
        for g in range(group):
            residual((b * group + g) * LANES)

    if ys > 1:
        for p in range(zs):
            across_wait(p).wait_recv()
    acc[...] = jnp.zeros_like(acc)

    @pl.loop(0, width // CHUNK)
    def _(j):
        dose = dose_all[:, :, :, :, lane_slice(j * CHUNK, CHUNK)].reshape(samples, CHUNK)
        real = dose.astype(F32)
        coef = dot(bt, dose, 1, 0)
        coef = coef[0:covs] + (coef[covs : 2 * covs] + coef[2 * covs :])
        sumsq = jnp.sum(real * real, axis=0, keepdims=True) - jnp.sum(
            coef * coef, axis=0, keepdims=True
        )
        scale = 1.0 / (sumsq + 0.1 * samples)
        twice = jnp.concatenate([dose, dose], axis=0)

        @pl.loop(0, gh // (group * LANES))
        def _(b):
            for g in range(group):
                at = pl.ds(pl.multiple_of((b * group + g) * LANES, LANES), LANES)
                cross = dot(pt[at, :], twice, 1, 0)
                chi = cross * cross * scale
                hit = 1.0 + jnp.tanh(chi - 4.0)
                acc[0, at, :] += sum(chi[:, i : i + LANES] for i in range(0, CHUNK, LANES))
                acc[1, at, :] += sum(hit[:, i : i + LANES] for i in range(0, CHUNK, LANES))

    line = lax.broadcasted_iota(jnp.int32, (8, 4 * LANES), 0)
    lane = lax.broadcasted_iota(jnp.int32, (8, 4 * LANES), 1)
    pick = (lane // (2 * LANES) == line).astype(F32).astype(BF16)

    def part_copy(j):
        return remote(
            part.at[j], landed.at[place], part_send.at[j], part_recv.at[place], y * peers + j
        )

    @pl.loop(0, peers)
    def _(j):
        at = pl.ds(pl.multiple_of(j * own, 8), own)
        terms = split(acc[0, at, :], 2) + split(acc[1, at, :], 2)
        sums = dot(pick, jnp.concatenate(terms, axis=1), 1, 1)
        part[j, :, pl.ds(0, own)] = sums[0:2, :]

        @pl.when(y * peers + j != me)
        def _():
            part_copy(j).start()

    @pl.when(me // peers == y)
    def _():
        landed[place] = part[lax.rem(me, peers)]

    for k in range(1, n):
        cov_copy(k).wait_send()
    if ys > 1:
        across().wait_send()
        for ci in range(cs):
            dose_across(ci).wait_send()
    if cs > 1:
        dose_copy(z, oc).wait_send()
        for p in range(zs):
            for d in range(ys):
                to_core(p, d).wait_send()
    for k in range(zs):
        for d in range(ys):
            @pl.when((z >= k) & (z + 1 < zs))
            def _():
                to_right(z - k, d).wait_send()

            @pl.when((z + k < zs) & (z > 0))
            def _():
                to_left(z + k, d).wait_send()

    def drained(p):
        for ci in range(cs):
            dose_copy(p, ci).wait_send()
        if ys > 1:
            dose_pass(p).wait_send()

    for k in range(1, zs):
        each_side(k, drained)
    for j in range(peers):
        @pl.when(y * peers + j != me)
        def _():
            part_copy(j).wait_send()

    for p in range(peers):
        src = index(p // cs, me // peers, p % cs)

        @pl.when(src != me)
        def _():
            remote(part.at[0], landed.at[p], part_send.at[0], part_recv.at[p], src).wait_recv()

    total = jnp.sum(landed[...], axis=0)
    kind = lax.broadcasted_iota(jnp.int32, total.shape, 0)
    out_ref[...] = jnp.where(kind == 0, total / variants, 10.0 / variants * total)


def local(dosage, covars, phenotypes):
    n = lax.axis_size("tile")
    rows, variants = dosage.shape
    genes = phenotypes.shape[1]
    covs = covars.shape[1]
    samples = rows * n
    cs = 2 if n % 2 == 0 else 1
    ys = 2 if n % (2 * cs) == 0 else 1
    zs = n // (cs * ys)
    peers = zs * cs
    gh = genes // ys
    own = genes // n
    width = variants // peers
    group = max(g for g in range(1, 8) if gh % (g * LANES) == 0)
    dma = pltpu.SemaphoreType.DMA
    out = pl.pallas_call(
        functools.partial(kernel, n, zs, ys, cs, own, group),
        out_shape=jax.ShapeDtypeStruct((2, LANES), F32),
        in_specs=[pl.BlockSpec(memory_space=pl.ANY)] * 3,
        out_specs=pl.BlockSpec(memory_space=pltpu.VMEM),
        scratch_shapes=[
            pltpu.VMEM((rows, variants), BF16),
            pltpu.VMEM((rows, gh), F32),
            dma((5,)),
            pltpu.VMEM((zs, cs, ys, rows, covs), F32),
            pltpu.VMEM((zs, cs, ys, rows, gh), F32),
            pltpu.VMEM((zs, cs, ys, rows, width), BF16),
            pltpu.VMEM((gh, 2 * samples), BF16),
            pltpu.VMEM((2, gh, LANES), F32),
            pltpu.VMEM((peers, 2, LANES), F32),
            pltpu.VMEM((peers, 2, LANES), F32),
            dma((n,)), dma((n,)), dma, dma,
            dma((zs, ys)), dma((zs, ys)), dma((zs, ys)), dma((zs, ys)), dma((zs,)),
            dma((zs, cs)), dma((cs,)), dma((zs,)), dma((zs,)), dma((zs,)),
            dma((peers,)), dma((peers,)),
        ],
        compiler_params=pltpu.CompilerParams(collective_id=0, has_side_effects=True),
    )(dosage, covars, phenotypes)
    return out[0, :own], out[1, :own]


def solution(mesh):
    spec = P(("cohort", "tile"), None)
    return jax.shard_map(
        local,
        mesh=mesh,
        in_specs=(spec, spec, spec),
        out_specs=(P(("cohort", "tile")), P(("cohort", "tile"))),
        check_vma=False,
    )
```

time: 33.4 us -> 36.7 us (1.099)
  Pallas kernels: 31.3 us -> 34.6 us
  other arithmetic: 1.25 us -> 0 us
  local copies, waits for them, and re-layouts: 0 us -> 1.25 us
    pallas_call x1, Pallas kernels: 31.3 us -> 34.6 us  [local(): pl.pallas_call(functools.partial(kernel, n, zs, ys, cs, own, group), out_...]
    mul x1 -> x0, other arithmetic: 1.25 us -> none  [local(): return (out[0, :own] / variants, 20.0 / variants * out[1, :own])]
    squeeze x0 -> x1, local copies, waits for them, and re-layouts: none -> 1.25 us  [local(): return (out[0, :own], out[1, :own])]
where the time goes in v1:
time: 36.7 us; the launch traced here: 36.5 us
  Pallas kernels  34.6 us (94%)
  local copies, waits for them, and re-layouts  1.25 us (3%)
  between operations  0.64 us (2%)
    pallas_call x1, Pallas kernels, local(): pl.pallas_call(functools.partial(kernel, n, zs, ys, cs, own, group), out_...  34.6 us
    squeeze x1, local copies, waits for them, and re-layouts, local(): return (out[0, :own], out[1, :own])  1.25 us

profile of v1, /device:TPU:0, one launch (start us, length us, event | category | flops | bytes accessed | tf_op | source)
XLA Modules:
  0.0 36.5 jit_solution(8869897694571665513)
XLA Ops:
  0.6 34.6 %shard_map.50 = f32[2,128]{1,0:T(2,128)} custom-call(bf16[16,8192]{1,0:T(8,128)(2,1)} %dose_in.1, f32[16,16]{1,0:T(8,128)} %cov_in.1, f32[16,1792]{1,0:T(8,128)} %pheno_in.1), custom_call_target="tpu_custom_call" | custom-call | tf_op jit(solution)/shard_map/pallas_call | solution.py:413
  35.2 1.3 %slice_bitcast_fusion = (f32[112]{0:T(128)}, f32[112]{0:T(128)}) fusion(f32[2,128]{1,0:T(2,128)} %shard_map.50), kind=kLoop, calls=%fused_computation | loop fusion | bytes 1792 | tf_op jit(solution)/shard_map/squeeze | solution.py:436

commit v2 on v1

v2 whole, which is shorter than its diff:
```python
import functools

import jax
import jax.numpy as jnp
from jax import lax
from jax.experimental import pallas as pl
from jax.experimental.pallas import tpu as pltpu
from jax.sharding import PartitionSpec as P

LANES = 128
CHUNK = 256
HIGH = lax.Precision.HIGHEST
F32 = jnp.float32
BF16 = jnp.bfloat16


def dot(a, b, ca, cb, precision=None):
    return lax.dot_general(
        a, b, (((ca,), (cb,)), ((), ())), precision=precision, preferred_element_type=F32
    )


def split(a, parts):
    out = []
    for _ in range(parts):
        term = a.astype(BF16)
        out.append(term)
        a = a - term.astype(F32)
    return out


def begin(copy):
    copy.start()


def sent(copy):
    copy.wait_send()


def inverse_factor(gram):
    size = gram.shape[0]
    wide = 2 * size
    row_id = lax.broadcasted_iota(jnp.int32, (size, wide), 0)
    eye = (
        lax.broadcasted_iota(jnp.int32, (size, size), 0)
        == lax.broadcasted_iota(jnp.int32, (size, size), 1)
    ).astype(F32)
    work = jnp.concatenate([gram, eye], axis=1)
    for k in range(0, size, 2):
        one = jnp.broadcast_to(work[:, k : k + 1], (size, wide))
        two = jnp.broadcast_to(work[:, k + 1 : k + 2], (size, wide))
        first = lax.rsqrt(one[k : k + 1, :])
        below = two[k : k + 1, :] * first
        second = lax.rsqrt(two[k + 1 : k + 2, :] - below * below)
        top = work[k : k + 1, :] * first
        low = (work[k + 1 : k + 2, :] - below * top) * second
        left = one * first
        right = (two - left * below) * second
        rest = work - left * top - right * low
        work = jnp.where(
            row_id > k + 1, rest, jnp.where(row_id == k, top, jnp.where(row_id == k + 1, low, work))
        )
    return work[:, size:]


def scan(
    c, y, z, oc, cs, ys, zs, n, owners, me, place, own, group, halves, hw, samples, covs,
    blocks, cut, cov_all, raw, dose_all, dres, vscale, pt, acc, part, landed, hand_on,
    each_side, cov_wait, pheno_wait, pheno_wait_own, resid_to, resid_pass, resid_wait,
    blocks_here, blocks_over, across_wait, d_recv, remote, part_copy, lane_slice,
):
    far = range(2, zs)
    hand_on(0, [1])

    for k in range(1, n):
        cov_wait(k).wait_recv()
    tiles = cov_all[...].reshape(n, 8, LANES)
    cov = jnp.concatenate(
        [tiles[:, :, i * covs : (i + 1) * covs] for i in range(samples // n // 8)], axis=1
    ).reshape(samples, covs)
    covt = cov.T
    factor = inverse_factor(dot(covt, cov, 1, 0, HIGH))
    basist = dot(factor, covt, 1, 0, HIGH)
    eye = (
        lax.broadcasted_iota(jnp.int32, (covs, covs), 0)
        == lax.broadcasted_iota(jnp.int32, (covs, covs), 1)
    ).astype(F32)
    fix = 1.5 * eye - 0.5 * dot(basist, basist, 1, 1, HIGH)
    basist = dot(fix, basist, 1, 0, HIGH)
    bt_hi, bt_mid, bt_low = [t.astype(F32) for t in split(basist, 3)]
    bt = jnp.concatenate([bt_hi, bt_mid, bt_low], axis=0).astype(BF16)
    b_hi, b_mid, b_low = [t.astype(F32) for t in split(basist.T, 3)]
    basis = jnp.concatenate([b_hi, b_hi, b_hi, b_mid, b_mid, b_low], axis=1).astype(BF16)

    def fitted(coef):
        one, two, three = [t.astype(F32) for t in split(coef, 3)]
        stack = jnp.concatenate([one, two, three, one, two, one], axis=0).astype(BF16)
        return dot(basis, stack, 1, 0)

    def dose_residual(h, j):
        cols = lane_slice(j * CHUNK, CHUNK)
        dose = dose_all[h, :, :, :, :, cols].reshape(samples, CHUNK)
        coef = dot(bt, dose, 1, 0)
        coef = coef[0:covs] + (coef[covs : 2 * covs] + coef[2 * covs :])
        resid = dose.astype(F32) - fitted(coef)
        dres[h, :, cols] = resid.astype(BF16)
        sumsq = jnp.sum(resid * resid, axis=0, keepdims=True)
        vscale[h, :, cols] = 1.0 / (sumsq + 0.1 * samples)

    def dose_residuals(h):
        if cs > 1:
            slot = dose_all.at[h, z, oc, y]
            remote(slot, slot, d_recv.at[h, z], d_recv.at[h, z], me).wait_recv()
        if ys > 1:
            for p in range(zs):
                across_wait(h, p).wait_recv()
        for j in range(hw // CHUNK):
            dose_residual(h, j)

    def arrived(p):
        for d in range(ys):
            pheno_wait(p, d)

    def residual(b, to):
        at = b * LANES
        pheno = raw[:, :, :, :, lane_slice(at, LANES)].reshape(samples, LANES)
        hi, mid, low = split(pheno, 3)
        with_hi = dot(bt, hi, 1, 0)
        with_mid = dot(bt[0 : 2 * covs], mid, 1, 0)
        coef = (
            with_hi[0:covs]
            + (with_hi[covs : 2 * covs] + with_mid[0:covs])
            + (with_hi[2 * covs :] + with_mid[covs:] + dot(bt[0:covs], low, 1, 0))
        )
        resid = pheno - fitted(coef)
        var = jnp.sum(resid * resid, axis=0, keepdims=True) / samples + 0.1
        pt[lane_slice(to * LANES, LANES), :] = (resid * lax.rsqrt(var)).astype(BF16).T

    def residuals():
        for i in range(cut):
            b = place * cut + i
            residual(jnp.minimum(b, blocks - 1), jnp.minimum(b, blocks))
        for i in range(cut):
            resid_to(i, begin)

    def pass_residuals():
        def body(b):
            resid_wait(b).wait_recv()
            if cs > 1:
                resid_pass(b).start()

        blocks_here(body)

    def wait_residuals(own_plane):
        if cs > 1:
            blocks_over(lambda b: resid_pass(b).wait_recv(), own_plane)

    mine = cs * cut
    soon = blocks - (blocks - 1) // mine * mine

    def associate(h, start, stop):
        wide = min(2 * CHUNK, hw)
        count = stop - start
        step = max(g for g in range(1, 8) if count % g == 0)

        @pl.loop(0, hw // wide)
        def _(j):
            cols = lane_slice(j * wide, wide)
            scale = vscale[h, :, cols]

            @pl.loop(0, count // step)
            def _(i):
                for g in range(step):
                    b = lax.rem(place // cs * mine + start + i * step + g, blocks)
                    at = lane_slice(b * LANES, LANES)
                    cross = dot(pt[at, :], dres[h, :, cols], 1, 0)
                    chi = cross * cross * scale
                    hit = 1.0 + jnp.tanh(chi - 4.0)
                    acc[0, at, :] += sum(chi[:, i : i + LANES] for i in range(0, wide, LANES))
                    acc[1, at, :] += sum(hit[:, i : i + LANES] for i in range(0, wide, LANES))

    acc[...] = jnp.zeros_like(acc)
    for h in range(1, halves):
        hand_on(h, [1])
    each_side(arrived)
    if cs > 1:
        for d in range(ys):
            pheno_wait_own(d)
    residuals()
    for h in range(halves):
        hand_on(h, far)
    dose_residuals(0)
    wait_residuals(True)
    associate(0, 0, soon)
    pass_residuals()
    for h in range(1, halves):
        dose_residuals(h)
        associate(h, 0, soon)
    wait_residuals(False)
    for h in range(halves):
        associate(h, soon, blocks)

    line = lax.broadcasted_iota(jnp.int32, (8, 4 * LANES), 0)
    lane = lax.broadcasted_iota(jnp.int32, (8, 4 * LANES), 1)
    pick = (lane // (2 * LANES) == line).astype(F32).astype(BF16)

    @pl.loop(0, owners // 8)
    def _(b):
        for i in range(8):
            j = b * 8 + i
            at = pl.ds(pl.multiple_of(j * own, 8), own)
            terms = split(acc[0, at, :], 2) + split(acc[1, at, :], 2)
            sums = dot(pick, jnp.concatenate(terms, axis=1), 1, 1)
            part[j, :, pl.ds(0, own)] = sums[0:2, :]
        for i in range(8):
            j = b * 8 + i

            @pl.when(y * owners + j != me)
            def _():
                part_copy(j).start()

    @pl.when(me // owners == y)
    def _():
        landed[place] = part[lax.rem(me, owners)]


def kernel(
    n, zs, ys, cs, lo, hi, own, group,
    dose_in, cov_in, pheno_in, out_ref,
    dose_ref, cov_ref, pheno_ref, load_sem, cov_all, raw, dose_all, dres, vscale, pt, acc, part, landed,
    cov_send, cov_recv, b_send, b_recv, a_send, a_core, a_recv,
    x_send, xo_send, x_recv, xc_send, xc_recv,
    d_send, dy_send, d_recv, pass_send, p_recv, part_send, part_recv,
):
    me = lax.axis_index("tile")
    rows, variants = dose_in.shape
    covs = cov_in.shape[1]
    samples = rows * n
    gh = raw.shape[-1]
    halves = dose_all.shape[0]
    hw = dose_all.shape[-1]
    width = halves * hw
    nc = hi - lo
    owners = n // ys
    c = lax.rem(me, cs)
    y = lax.rem(me // cs, ys)
    z = me // (cs * ys)
    oc = lax.rem(c + 1, cs)
    oy = lax.rem(y + 1, ys)
    place = (z - lo) * cs + c
    mid = (z >= lo) & (z < hi)
    far = (2 * z) // zs

    def index(zi, yi, ci):
        return (zi * ys + yi) * cs + ci

    def remote(src, dst, ssem, rsem, dev):
        return pltpu.make_async_remote_copy(
            src_ref=src, dst_ref=dst, send_sem=ssem, recv_sem=rsem,
            device_id={"tile": dev}, device_id_type=pl.DeviceIdType.MESH,
        )

    def lane_slice(start, size):
        return pl.ds(pl.multiple_of(start, LANES), size)

    loads = [
        pltpu.make_async_copy(cov_in, cov_ref, load_sem.at[0]),
        pltpu.make_async_copy(
            pheno_in.at[:, lane_slice(oy * gh, gh)], pheno_ref, load_sem.at[2]
        ),
        pltpu.make_async_copy(
            pheno_in.at[:, lane_slice(y * gh, gh)], raw.at[z, c, y], load_sem.at[1]
        ),
        pltpu.make_async_copy(dose_in, dose_ref, load_sem.at[3]),
    ]

    def own_dose(h):
        return pltpu.make_async_copy(
            dose_in.at[:, lane_slice(place * width + h * hw, hw)],
            dose_all.at[h, z, c, y], load_sem.at[4 + h],
        )

    for load in loads:
        load.start()

    @pl.when(mid)
    def _():
        for h in range(halves):
            own_dose(h).start()

    barrier = pltpu.get_barrier_semaphore()

    def greet(dev):
        pl.semaphore_signal(
            barrier, inc=1, device_id={"tile": dev}, device_id_type=pl.DeviceIdType.MESH
        )

    @pl.when(mid)
    def _():
        for k in range(1, n):
            greet(lax.rem(me + k, n))

    if ys > 1:
        @pl.when(jnp.logical_not(mid))
        def _():
            greet(index(z, oy, c))

    for load in loads:
        load.wait()
    packed = [cov_ref[g : g + 8, :] for g in range(0, rows, 8)]
    fill = jnp.zeros((8, LANES - len(packed) * covs), F32)
    cov_all[z, c, y] = jnp.concatenate(packed + [fill], axis=1)

    @pl.when(mid)
    def _():
        for h in range(halves):
            own_dose(h).wait()
        pl.semaphore_wait(barrier, nc * ys * cs - 1)

    @pl.when(jnp.logical_not(mid))
    def _():
        pl.semaphore_wait(barrier, nc * ys * cs + (1 if ys > 1 else 0))

    def plane(i, body):
        p = jnp.where(mid, lo + lax.rem(z - lo + 1 + i + nc, nc), lo + i + far * (nc - 1 - 2 * i))

        @pl.when(p != z)
        def _():
            body(p)

    def planes(body):
        for i in range(nc):
            plane(i, body)

    def cov_copies(act):
        own_cov = cov_all.at[z, c, y]
        for j in range(nc * ys * cs):
            dev = lo * ys * cs + j

            @pl.when(dev != me)
            def _():
                act(remote(own_cov, own_cov, cov_send.at[j], cov_recv.at[me], dev))

    def cov_wait(k):
        src = lax.rem(me + n - k, n)
        slot = cov_all.at[src // (cs * ys), lax.rem(src, cs), lax.rem(src // cs, ys)]
        return remote(slot, slot, cov_send.at[0], cov_recv.at[src], me)

    def across():
        return remote(pheno_ref, raw.at[z, c, y], b_send, b_recv, index(z, oy, c))

    blocks = gh // LANES
    cut = -(-blocks // (nc * cs))

    def first(q):
        return jnp.minimum(q * cut, blocks - cut)

    def raw_slot(p, ci, d, q):
        return raw.at[p, ci, lax.rem(y + d, ys), :, lane_slice(first(q) * LANES, cut * LANES)]

    def pheno_to(d, act):
        def to(p):
            for ci in range(cs):
                slot = raw_slot(z, c, d, (p - lo) * cs + ci)
                act(
                    remote(
                        slot, slot, a_send.at[p - lo, ci, d], a_recv.at[z, d], index(p, y, ci)
                    )
                )

        return to

    def pheno_over(d, act):
        if cs > 1:
            @pl.when(mid)
            def _():
                slot = raw_slot(z, c, d, (z - lo) * cs + oc)
                act(remote(slot, slot, a_core.at[d], a_recv.at[z, d], index(z, y, oc)))

    def pheno_wait(p, d):
        slot = raw_slot(p, pl.ds(0, cs), d, place)
        remote(slot, slot, a_core.at[d], a_recv.at[p, d], me).wait_recv()

    def pheno_wait_own(d):
        slot = raw_slot(z, oc, d, place)
        remote(slot, slot, a_core.at[d], a_recv.at[z, d], me).wait_recv()

    def resid_slot(b):
        return pt.at[pl.ds(pl.multiple_of(b * LANES, LANES), LANES)]

    def resid_to(i, act):
        b = place * cut + i

        @pl.when(b < blocks)
        def _():
            for j in range(1, nc):
                p = lo + lax.rem(z - lo + j, nc)
                act(
                    remote(
                        resid_slot(b), resid_slot(b), x_send.at[i, j], x_recv.at[b], index(p, y, c)
                    )
                )
            if cs > 1:
                act(
                    remote(
                        resid_slot(b), resid_slot(b), xo_send.at[i], xc_recv.at[b], index(z, y, oc)
                    )
                )

    def resid_pass(b):
        return remote(
            resid_slot(b), resid_slot(b), xc_send.at[b], xc_recv.at[b], index(z, y, oc)
        )

    def resid_wait(b):
        return remote(resid_slot(b), resid_slot(b), xc_send.at[b], x_recv.at[b], me)

    def blocks_here(body):
        for b in range(blocks):
            q = b // cut

            @pl.when((c == q % cs) & (z != lo + q // cs))
            def _():
                body(b)

    def blocks_over(body, own_plane):
        for b in range(blocks):
            q = b // cut
            near = z == lo + q // cs

            @pl.when((c != q % cs) & (near if own_plane else jnp.logical_not(near)))
            def _():
                body(b)

    def block(p, ci, h):
        return dose_ref.at[:, lane_slice(((p - lo) * cs + ci) * width + h * hw, hw)]

    def dose_to(h, act):
        def to(p):
            for ci in range(cs):
                act(
                    remote(
                        block(p, ci, h), dose_all.at[h, z, c, y],
                        d_send.at[h, p - lo, ci], d_recv.at[h, z], index(p, y, ci),
                    )
                )

        return to

    def own_copies(h, act):
        @pl.when(mid)
        def _():
            if ys > 1:
                for ci in range(cs):
                    act(
                        remote(
                            block(z, ci, h), dose_all.at[h, z, c, y],
                            dy_send.at[h, ci], p_recv.at[h, z], index(z, oy, ci),
                        )
                    )
            if cs > 1:
                act(
                    remote(
                        block(z, oc, h), dose_all.at[h, z, c, y],
                        d_send.at[h, z - lo, oc], d_recv.at[h, z], index(z, y, oc),
                    )
                )

    def dose_pass(h, p):
        slot = dose_all.at[h, p, :, y]
        return remote(slot, slot, pass_send.at[h, p], p_recv.at[h, p], index(z, oy, c))

    def dose_wait(h, p):
        slot = dose_all.at[h, p, :, y]
        return remote(slot, slot, pass_send.at[h, p], d_recv.at[h, p], me)

    def across_wait(h, p):
        slot = dose_all.at[h, p, :, oy]
        return remote(slot, slot, pass_send.at[h, p], p_recv.at[h, p], me)

    def at_distance(k, body):
        @pl.when(z >= k)
        def _():
            body(z - k)

        @pl.when(z + k < zs)
        def _():
            body(z + k)

    def each_side(body):
        for k in range(1, zs):
            at_distance(k, body)

    def hand_on(h, ks):
        def body(p):
            dose_wait(h, p).wait_recv()
            if ys > 1:
                dose_pass(h, p).start()

        for k in ks:
            at_distance(k, body)

    if ys > 1:
        across().start()
    own_copies(0, begin)
    plane(0, dose_to(0, begin))
    cov_copies(begin)
    for h in range(1, halves):
        own_copies(h, begin)
        plane(0, dose_to(h, begin))
    pheno_over(0, begin)
    for i in range(nc):
        plane(i, pheno_to(0, begin))
    if ys > 1:
        slot = raw.at[z, c, oy]
        remote(slot, slot, b_send, b_recv, me).wait_recv()
        pheno_over(1, begin)
        for i in range(nc):
            plane(i, pheno_to(1, begin))
    for i in range(1, nc):
        for h in range(halves):
            plane(i, dose_to(h, begin))

    def part_copy(j):
        return remote(
            part.at[j], landed.at[place], part_send.at[j], part_recv.at[place], y * owners + j
        )

    @pl.when(mid)
    def _():
        scan(
            c, y, z, oc, cs, ys, zs, n, owners, me, place, own, group, halves, hw, samples,
            covs, blocks, cut, cov_all, raw, dose_all, dres, vscale, pt, acc, part, landed,
            hand_on, each_side, cov_wait, pheno_wait, pheno_wait_own, resid_to,
            resid_pass, resid_wait, blocks_here, blocks_over, across_wait, d_recv, remote, part_copy,
            lane_slice,
        )

    if ys > 1:
        across().wait_send()
    cov_copies(sent)
    for d in range(ys):
        pheno_over(d, sent)
        planes(pheno_to(d, sent))
    for h in range(halves):
        own_copies(h, sent)
        planes(dose_to(h, sent))

    @pl.when(mid)
    def _():
        for i in range(cut):
            resid_to(i, sent)
        if cs > 1:
            blocks_here(lambda b: resid_pass(b).wait_send())
        if ys > 1:
            for h in range(halves):
                each_side(lambda p: dose_pass(h, p).wait_send())

    for p in range(nc * cs):
        src = index(lo + p // cs, me // owners, p % cs)

        @pl.when(src != me)
        def _():
            remote(part.at[0], landed.at[p], part_send.at[0], part_recv.at[p], me).wait_recv()

    total = jnp.sum(landed[...], axis=0)
    kind = lax.broadcasted_iota(jnp.int32, total.shape, 0)
    out_ref[...] = jnp.where(kind == 0, total / variants, 10.0 / variants * total)

    @pl.when(mid)
    def _():
        for j in range(owners):
            @pl.when(y * owners + j != me)
            def _():
                part_copy(j).wait_send()


def local(dosage, covars, phenotypes):
    n = lax.axis_size("tile")
    rows, variants = dosage.shape
    genes = phenotypes.shape[1]
    covs = covars.shape[1]
    samples = rows * n
    cs = 2 if n % 2 == 0 else 1
    ys = 2 if n % (2 * cs) == 0 else 1
    zs = n // (cs * ys)
    lo, hi = zs // 4, zs - zs // 4
    peers = (hi - lo) * cs
    owners = n // ys
    gh = genes // ys
    own = genes // n
    halves = 2
    hw = variants // peers // halves
    blocks = gh // LANES
    group = max(g for g in range(1, 8) if blocks % g == 0)
    dma = pltpu.SemaphoreType.DMA
    out = pl.pallas_call(
        functools.partial(kernel, n, zs, ys, cs, lo, hi, own, group),
        out_shape=pltpu.VMEM((2, LANES), F32),
        in_specs=[pl.BlockSpec(memory_space=pl.ANY)] * 3,
        out_specs=pl.BlockSpec(memory_space=pltpu.VMEM),
        scratch_shapes=[
            pltpu.VMEM((rows, variants), BF16),
            pltpu.VMEM((rows, covs), F32),
            pltpu.VMEM((rows, gh), F32),
            dma((4 + halves,)),
            pltpu.VMEM((zs, cs, ys, 8, LANES), F32),
            pltpu.VMEM((zs, cs, ys, rows, gh), F32),
            pltpu.VMEM((halves, zs, cs, ys, rows, hw), BF16),
            pltpu.VMEM((halves, samples, hw), BF16),
            pltpu.VMEM((halves, 1, hw), F32),
            pltpu.VMEM((gh + LANES, samples), BF16),
            pltpu.VMEM((2, gh, LANES), F32),
            pltpu.VMEM((owners, 2, LANES), F32),
            pltpu.VMEM((peers, 2, LANES), F32),
            dma((n,)), dma((n,)), dma, dma,
            dma((hi - lo, cs, ys)), dma((ys,)), dma((zs, ys)),
            dma((blocks, hi - lo)), dma((blocks,)), dma((blocks,)), dma((blocks,)), dma((blocks,)),
            dma((halves, hi - lo, cs)), dma((halves, cs)), dma((halves, zs)),
            dma((halves, zs)), dma((halves, zs)),
            dma((owners,)), dma((peers,)),
        ],
        compiler_params=pltpu.CompilerParams(collective_id=0, has_side_effects=True),
    )(dosage, covars, phenotypes)
    return out[0, :own], out[1, :own]


def solution(mesh):
    spec = P(("cohort", "tile"), None)
    return jax.shard_map(
        local,
        mesh=mesh,
        in_specs=(spec, spec, spec),
        out_specs=(P(("cohort", "tile")), P(("cohort", "tile"))),
        check_vma=False,
    )
```

time: 36.7 us -> 29.3 us (0.80)
  Pallas kernels: 34.6 us -> 27.9 us
  local copies, waits for them, and re-layouts: 1.25 us -> 0.52 us
    pallas_call x1, Pallas kernels: 34.6 us -> 27.9 us  [local(): pl.pallas_call(functools.partial(kernel, n, zs, ys, cs, lo, hi, own, grou...]
    squeeze x1, local copies, waits for them, and re-layouts: 1.25 us -> 0.52 us  [local(): return (out[0, :own], out[1, :own])]
where the time goes in v2:
time: 29.3 us; the launch traced here: 29 us
  Pallas kernels  27.9 us (95%)
  between operations  0.64 us (2%)
  local copies, waits for them, and re-layouts  0.52 us (2%)
    pallas_call x1, Pallas kernels, local(): pl.pallas_call(functools.partial(kernel, n, zs, ys, cs, lo, hi, own, grou...  27.9 us

profile of v2, /device:TPU:0, one launch (start us, length us, event | category | flops | bytes accessed | tf_op | source)
XLA Modules:
  0.0 29.0 jit_solution(8223884600293881529)
XLA Ops:
  0.6 27.9 %shard_map.50 = f32[2,128]{1,0:T(2,128)S(1)} custom-call(bf16[16,8192]{1,0:T(8,128)(2,1)} %dose_in.1, f32[16,16]{1,0:T(8,128)} %cov_in.1, f32[16,1792]{1,0:T(8,128)} %pheno_in.1), custom_call_target="tpu_custom_call" | custom-call | tf_op jit(solution)/shard_map/pallas_call | solution.py:597
  28.5 0.5 %slice_bitcast_fusion = (f32[112]{0:T(128)}, f32[112]{0:T(128)}) fusion(f32[2,128]{1,0:T(2,128)S(1)} %shard_map.50), kind=kLoop, calls=%fused_computation | loop fusion | bytes 1792 | tf_op jit(solution)/shard_map/squeeze | solution.py:625

commit v3 on v2

--- a/solution.py
+++ b/solution.py
@@ -27,14 +27,6 @@
         out.append(term)
         a = a - term.astype(F32)
     return out
-
-
-def begin(copy):
-    copy.start()
-
-
-def sent(copy):
-    copy.wait_send()
 
 
 def inverse_factor(gram):
@@ -64,17 +56,16 @@
 
 
 def scan(
-    c, y, z, oc, cs, ys, zs, n, owners, me, place, own, group, halves, hw, samples, covs,
-    blocks, cut, cov_all, raw, dose_all, dres, vscale, pt, acc, part, landed, hand_on,
-    each_side, cov_wait, pheno_wait, pheno_wait_own, resid_to, resid_pass, resid_wait,
-    blocks_here, blocks_over, across_wait, d_recv, remote, part_copy, lane_slice,
+    c, y, z, oc, other_row, cs, ys, zs, n, owners, me, place, own, halves, hw, samples, covs,
+    blocks, cut, cov_all, raw, dose_all, dres, vscale, pt, acc, part, landed, hand_on, cov_wait,
+    pheno_wait, resid_to, resid_pass, resid_wait, blocks_here, blocks_over, across_wait, d_recv,
+    remote, send_part, in_group, lane_slice,
 ):
     far = range(2, zs)
     hand_on(0, [1])
 
-    for k in range(1, n):
-        cov_wait(k).wait_recv()
-    tiles = cov_all[...].reshape(n, 8, LANES)
+    cov_wait(n - 1)
+    tiles = cov_all[...]
     cov = jnp.concatenate(
         [tiles[:, :, i * covs : (i + 1) * covs] for i in range(samples // n // 8)], axis=1
     ).reshape(samples, covs)
@@ -99,7 +90,7 @@
 
     def dose_residual(h, j):
         cols = lane_slice(j * CHUNK, CHUNK)
-        dose = dose_all[h, :, :, :, :, cols].reshape(samples, CHUNK)
+        dose = dose_all[h, :, :, :, cols].reshape(samples, CHUNK)
         coef = dot(bt, dose, 1, 0)
         coef = coef[0:covs] + (coef[covs : 2 * covs] + coef[2 * covs :])
         resid = dose.astype(F32) - fitted(coef)
@@ -109,21 +100,16 @@
 
     def dose_residuals(h):
         if cs > 1:
-            slot = dose_all.at[h, z, oc, y]
+            slot = dose_all.at[h, other_row, y]
             remote(slot, slot, d_recv.at[h, z], d_recv.at[h, z], me).wait_recv()
         if ys > 1:
-            for p in range(zs):
-                across_wait(h, p).wait_recv()
+            across_wait(h)
         for j in range(hw // CHUNK):
             dose_residual(h, j)
 
-    def arrived(p):
-        for d in range(ys):
-            pheno_wait(p, d)
-
     def residual(b, to):
         at = b * LANES
-        pheno = raw[:, :, :, :, lane_slice(at, LANES)].reshape(samples, LANES)
+        pheno = raw[:, :, :, lane_slice(at, LANES)].reshape(samples, LANES)
         hi, mid, low = split(pheno, 3)
         with_hi = dot(bt, hi, 1, 0)
         with_mid = dot(bt[0 : 2 * covs], mid, 1, 0)
@@ -141,7 +127,7 @@
             b = place * cut + i
             residual(jnp.minimum(b, blocks - 1), jnp.minimum(b, blocks))
         for i in range(cut):
-            resid_to(i, begin)
+            resid_to(i)
 
     def pass_residuals():
         def body(b):
@@ -182,10 +168,7 @@
     acc[...] = jnp.zeros_like(acc)
     for h in range(1, halves):
         hand_on(h, [1])
-    each_side(arrived)
-    if cs > 1:
-        for d in range(ys):
-            pheno_wait_own(d)
+    pheno_wait(zs * cs - 1)
     residuals()
     for h in range(halves):
         hand_on(h, far)
@@ -217,20 +200,18 @@
 
             @pl.when(y * owners + j != me)
             def _():
-                part_copy(j).start()
-
-    @pl.when(me // owners == y)
+                send_part(j)
+
+    @pl.when(in_group)
     def _():
         landed[place] = part[lax.rem(me, owners)]
 
 
 def kernel(
-    n, zs, ys, cs, lo, hi, own, group,
+    n, zs, ys, cs, lo, hi, own,
     dose_in, cov_in, pheno_in, out_ref,
-    dose_ref, cov_ref, pheno_ref, load_sem, cov_all, raw, dose_all, dres, vscale, pt, acc, part, landed,
-    cov_send, cov_recv, b_send, b_recv, a_send, a_core, a_recv,
-    x_send, xo_send, x_recv, xc_send, xc_recv,
-    d_send, dy_send, d_recv, pass_send, p_recv, part_send, part_recv,
+    dose_ref, cov_ref, pheno_ref, load_sem, sends, cov_all, raw, dose_all, dres, vscale, pt, acc,
+    part, landed, recvs, x_sem, d_recv, p_recv,
 ):
     me = lax.axis_index("tile")
     rows, variants = dose_in.shape
@@ -248,6 +229,10 @@
     oc = lax.rem(c + 1, cs)
     oy = lax.rem(y + 1, ys)
     place = (z - lo) * cs + c
+    own_row = z * cs + c
+    other_row = z * cs + oc
+    cov_send, b_send, a_send, d_send, pass_send, part_send, xc_send = [sends.at[i] for i in range(7)]
+    cov_recv, b_recv, a_recv, part_recv = [recvs.at[i] for i in range(4)]
     mid = (z >= lo) & (z < hi)
     far = (2 * z) // zs
 
@@ -269,7 +254,7 @@
             pheno_in.at[:, lane_slice(oy * gh, gh)], pheno_ref, load_sem.at[2]
         ),
         pltpu.make_async_copy(
-            pheno_in.at[:, lane_slice(y * gh, gh)], raw.at[z, c, y], load_sem.at[1]
+            pheno_in.at[:, lane_slice(y * gh, gh)], raw.at[own_row, y], load_sem.at[1]
         ),
         pltpu.make_async_copy(dose_in, dose_ref, load_sem.at[3]),
     ]
@@ -277,7 +262,7 @@
     def own_dose(h):
         return pltpu.make_async_copy(
             dose_in.at[:, lane_slice(place * width + h * hw, hw)],
-            dose_all.at[h, z, c, y], load_sem.at[4 + h],
+            dose_all.at[h, own_row, y], load_sem.at[4 + h],
         )
 
     for load in loads:
@@ -309,7 +294,7 @@
         load.wait()
     packed = [cov_ref[g : g + 8, :] for g in range(0, rows, 8)]
     fill = jnp.zeros((8, LANES - len(packed) * covs), F32)
-    cov_all[z, c, y] = jnp.concatenate(packed + [fill], axis=1)
+    cov_all[own_row * ys + y] = jnp.concatenate(packed + [fill], axis=1)
 
     @pl.when(mid)
     def _():
@@ -332,22 +317,25 @@
         for i in range(nc):
             plane(i, body)
 
-    def cov_copies(act):
-        own_cov = cov_all.at[z, c, y]
+    def cov_copies():
+        own_cov = cov_all.at[own_row * ys + y]
         for j in range(nc * ys * cs):
             dev = lo * ys * cs + j
 
             @pl.when(dev != me)
             def _():
-                act(remote(own_cov, own_cov, cov_send.at[j], cov_recv.at[me], dev))
-
-    def cov_wait(k):
-        src = lax.rem(me + n - k, n)
-        slot = cov_all.at[src // (cs * ys), lax.rem(src, cs), lax.rem(src // cs, ys)]
-        return remote(slot, slot, cov_send.at[0], cov_recv.at[src], me)
+                remote(own_cov, own_cov, cov_send, cov_recv, dev).start()
+
+    def cov_wait(count, send=False):
+        slot = cov_all.at[pl.ds(0, count)]
+        copy = remote(slot, slot, cov_send, cov_recv, me)
+        if send:
+            copy.wait_send()
+        else:
+            copy.wait_recv()
 
     def across():
-        return remote(pheno_ref, raw.at[z, c, y], b_send, b_recv, index(z, oy, c))
+        return remote(pheno_ref, raw.at[own_row, y], b_send, b_recv, index(z, oy, c))
 
     blocks = gh // LANES
     cut = -(-blocks // (nc * cs))
@@ -355,65 +343,69 @@
     def first(q):
         return jnp.minimum(q * cut, blocks - cut)
 
-    def raw_slot(p, ci, d, q):
-        return raw.at[p, ci, lax.rem(y + d, ys), :, lane_slice(first(q) * LANES, cut * LANES)]
-
-    def pheno_to(d, act):
+    def raw_slot(d, q):
+        lanes = lane_slice(first(q) * LANES, cut * LANES)
+        return raw.at[own_row, lax.rem(y + d, ys), :, lanes]
+
+    def pheno_to(d):
         def to(p):
             for ci in range(cs):
-                slot = raw_slot(z, c, d, (p - lo) * cs + ci)
-                act(
-                    remote(
-                        slot, slot, a_send.at[p - lo, ci, d], a_recv.at[z, d], index(p, y, ci)
-                    )
-                )
+                slot = raw_slot(d, (p - lo) * cs + ci)
+                remote(slot, slot, a_send, a_recv, index(p, y, ci)).start()
 
         return to
 
-    def pheno_over(d, act):
+    def pheno_over(d):
         if cs > 1:
             @pl.when(mid)
             def _():
-                slot = raw_slot(z, c, d, (z - lo) * cs + oc)
-                act(remote(slot, slot, a_core.at[d], a_recv.at[z, d], index(z, y, oc)))
-
-    def pheno_wait(p, d):
-        slot = raw_slot(p, pl.ds(0, cs), d, place)
-        remote(slot, slot, a_core.at[d], a_recv.at[p, d], me).wait_recv()
-
-    def pheno_wait_own(d):
-        slot = raw_slot(z, oc, d, place)
-        remote(slot, slot, a_core.at[d], a_recv.at[z, d], me).wait_recv()
+                slot = raw_slot(d, (z - lo) * cs + oc)
+                remote(slot, slot, a_send, a_recv, index(z, y, oc)).start()
+
+    def pheno_wait(count, send=False):
+        slot = raw.at[pl.ds(0, count), :, :, pl.ds(0, cut * LANES)]
+        copy = remote(slot, slot, a_send, a_recv, me)
+        if send:
+            copy.wait_send()
+        else:
+            copy.wait_recv()
 
     def resid_slot(b):
         return pt.at[pl.ds(pl.multiple_of(b * LANES, LANES), LANES)]
 
-    def resid_to(i, act):
+    def resid_to(i):
         b = place * cut + i
 
         @pl.when(b < blocks)
         def _():
             for j in range(1, nc):
                 p = lo + lax.rem(z - lo + j, nc)
-                act(
-                    remote(
-                        resid_slot(b), resid_slot(b), x_send.at[i, j], x_recv.at[b], index(p, y, c)
-                    )
-                )
+                remote(
+                    resid_slot(b), resid_slot(b), x_sem.at[0, 0, i], x_sem.at[z - lo, 1, i],
+                    index(p, y, c),
+                ).start()
             if cs > 1:
-                act(
-                    remote(
-                        resid_slot(b), resid_slot(b), xo_send.at[i], xc_recv.at[b], index(z, y, oc)
-                    )
-                )
+                remote(
+                    resid_slot(b), resid_slot(b), x_sem.at[0, 0, i], x_sem.at[z - lo, 2, i],
+                    index(z, y, oc),
+                ).start()
+
+    def resid_sent(i):
+        slot = pt.at[pl.ds(0, (nc - 1 + (1 if cs > 1 else 0)) * LANES)]
+
+        @pl.when(place * cut + i < blocks)
+        def _():
+            remote(slot, slot, x_sem.at[0, 0, i], x_sem.at[0, 1, i], me).wait_send()
 
     def resid_pass(b):
+        source = b // cut // cs
         return remote(
-            resid_slot(b), resid_slot(b), xc_send.at[b], xc_recv.at[b], index(z, y, oc)
+            resid_slot(b), resid_slot(b), xc_send, x_sem.at[source, 2, b % cut], index(z, y, oc)
         )
 
     def resid_wait(b):
-        return remote(resid_slot(b), resid_slot(b), xc_send.at[b], x_recv.at[b], me)
+        source = b // cut // cs
+        return remote(resid_slot(b), resid_slot(b), xc_send, x_sem.at[source, 1, b % cut], me)
 
     def blocks_here(body):
         for b in range(blocks):
@@ -432,51 +424,64 @@
             def _():
                 body(b)
 
+    def passed_all():
+        for at in range(nc):
+            for ci in range(cs):
+                count = sum(b // cut % cs == ci and b // cut // cs != at for b in range(blocks))
+                if count:
+                    slot = pt.at[pl.ds(0, count * LANES)]
+
+                    @pl.when((z == lo + at) & (c == ci))
+                    def _():
+                        remote(slot, slot, xc_send, xc_send, me).wait_send()
+
     def block(p, ci, h):
         return dose_ref.at[:, lane_slice(((p - lo) * cs + ci) * width + h * hw, hw)]
 
-    def dose_to(h, act):
+    def dose_to(h):
         def to(p):
             for ci in range(cs):
-                act(
-                    remote(
-                        block(p, ci, h), dose_all.at[h, z, c, y],
-                        d_send.at[h, p - lo, ci], d_recv.at[h, z], index(p, y, ci),
-                    )
-                )
+                remote(
+                    block(p, ci, h), dose_all.at[h, own_row, y], d_send, d_recv.at[h, z],
+                    index(p, y, ci),
+                ).start()
 
         return to
 
-    def own_copies(h, act):
+    def own_copies(h):
         @pl.when(mid)
         def _():
             if ys > 1:
                 for ci in range(cs):
-                    act(
-                        remote(
-                            block(z, ci, h), dose_all.at[h, z, c, y],
-                            dy_send.at[h, ci], p_recv.at[h, z], index(z, oy, ci),
-                        )
-                    )
+                    remote(
+                        block(z, ci, h), dose_all.at[h, own_row, y], d_send, p_recv.at[h],
+                        index(z, oy, ci),
+                    ).start()
             if cs > 1:
-                act(
-                    remote(
-                        block(z, oc, h), dose_all.at[h, z, c, y],
-                        d_send.at[h, z - lo, oc], d_recv.at[h, z], index(z, y, oc),
-                    )
-                )
+                remote(
+                    block(z, oc, h), dose_all.at[h, own_row, y], d_send, d_recv.at[h, z],
+                    index(z, y, oc),
+                ).start()
+
+    def dose_sent(count):
+        slot = dose_all.at[:, pl.ds(0, count), 0]
+        remote(slot, slot, d_send, d_recv.at[0, 0], me).wait_send()
 
     def dose_pass(h, p):
-        slot = dose_all.at[h, p, :, y]
-        return remote(slot, slot, pass_send.at[h, p], p_recv.at[h, p], index(z, oy, c))
+        slot = dose_all.at[h, pl.ds(p * cs, cs), y]
+        return remote(slot, slot, pass_send, p_recv.at[h], index(z, oy, c))
+
+    def passes_sent():
+        slot = dose_all.at[:, pl.ds(0, (zs - 1) * cs), 0]
+        remote(slot, slot, pass_send, p_recv.at[0], me).wait_send()
 
     def dose_wait(h, p):
-        slot = dose_all.at[h, p, :, y]
-        return remote(slot, slot, pass_send.at[h, p], d_recv.at[h, p], me)
-
-    def across_wait(h, p):
-        slot = dose_all.at[h, p, :, oy]
-        return remote(slot, slot, pass_send.at[h, p], p_recv.at[h, p], me)
+        slot = dose_all.at[h, pl.ds(p * cs, cs), y]
+        return remote(slot, slot, pass_send, d_recv.at[h, p], me)
+
+    def across_wait(h):
+        slot = dose_all.at[h, :, oy]
+        remote(slot, slot, pass_send, p_recv.at[h], me).wait_recv()
 
     def at_distance(k, body):
         @pl.when(z >= k)
@@ -486,10 +491,6 @@
         @pl.when(z + k < zs)
         def _():
             body(z + k)
-
-    def each_side(body):
-        for k in range(1, zs):
-            at_distance(k, body)
 
     def hand_on(h, ks):
         def body(p):
@@ -502,77 +503,86 @@
 
     if ys > 1:
         across().start()
-    own_copies(0, begin)
-    plane(0, dose_to(0, begin))
-    cov_copies(begin)
+    own_copies(0)
+    plane(0, dose_to(0))
+    cov_copies()
     for h in range(1, halves):
-        own_copies(h, begin)
-        plane(0, dose_to(h, begin))
-    pheno_over(0, begin)
+        own_copies(h)
+        plane(0, dose_to(h))
+    pheno_over(0)
     for i in range(nc):
-        plane(i, pheno_to(0, begin))
+        plane(i, pheno_to(0))
     if ys > 1:
-        slot = raw.at[z, c, oy]
+        slot = raw.at[own_row, oy]
         remote(slot, slot, b_send, b_recv, me).wait_recv()
-        pheno_over(1, begin)
+        pheno_over(1)
         for i in range(nc):
-            plane(i, pheno_to(1, begin))
+            plane(i, pheno_to(1))
     for i in range(1, nc):
         for h in range(halves):
-            plane(i, dose_to(h, begin))
-
-    def part_copy(j):
-        return remote(
-            part.at[j], landed.at[place], part_send.at[j], part_recv.at[place], y * owners + j
-        )
+            plane(i, dose_to(h))
+
+    in_group = mid & (me // owners == y)
+
+    def send_part(j):
+        remote(part.at[j], landed.at[place], part_send, part_recv, y * owners + j).start()
 
     @pl.when(mid)
     def _():
         scan(
-            c, y, z, oc, cs, ys, zs, n, owners, me, place, own, group, halves, hw, samples,
+            c, y, z, oc, other_row, cs, ys, zs, n, owners, me, place, own, halves, hw, samples,
             covs, blocks, cut, cov_all, raw, dose_all, dres, vscale, pt, acc, part, landed,
-            hand_on, each_side, cov_wait, pheno_wait, pheno_wait_own, resid_to,
-            resid_pass, resid_wait, blocks_here, blocks_over, across_wait, d_recv, remote, part_copy,
-            lane_slice,
+            hand_on, cov_wait, pheno_wait, resid_to, resid_pass, resid_wait, blocks_here,
+            blocks_over, across_wait, d_recv, remote, send_part, in_group, lane_slice,
         )
 
     if ys > 1:
         across().wait_send()
-    cov_copies(sent)
-    for d in range(ys):
-        pheno_over(d, sent)
-        planes(pheno_to(d, sent))
-    for h in range(halves):
-        own_copies(h, sent)
-        planes(dose_to(h, sent))
 
     @pl.when(mid)
     def _():
+        cov_wait(nc * ys * cs - 1, send=True)
+        pheno_wait((nc - 1) * cs + (1 if cs > 1 else 0), send=True)
+        dose_sent((nc - 1) * cs + (cs if ys > 1 else 0) + (1 if cs > 1 else 0))
+        if ys > 1:
+            passes_sent()
         for i in range(cut):
-            resid_to(i, sent)
-        if cs > 1:
-            blocks_here(lambda b: resid_pass(b).wait_send())
-        if ys > 1:
-            for h in range(halves):
-                each_side(lambda p: dose_pass(h, p).wait_send())
-
-    for p in range(nc * cs):
-        src = index(lo + p // cs, me // owners, p % cs)
-
-        @pl.when(src != me)
-        def _():
-            remote(part.at[0], landed.at[p], part_send.at[0], part_recv.at[p], me).wait_recv()
+            resid_sent(i)
+        passed_all()
+
+    @pl.when(jnp.logical_not(mid))
+    def _():
+        cov_wait(nc * ys * cs, send=True)
+        pheno_wait(nc * cs, send=True)
+        dose_sent(nc * cs)
+
+    def parts_landed(count):
+        slot = landed.at[pl.ds(0, count)]
+        remote(slot, slot, part_send, part_recv, me).wait_recv()
+
+    @pl.when(in_group)
+    def _():
+        parts_landed(nc * cs - 1)
+
+    @pl.when(jnp.logical_not(in_group))
+    def _():
+        parts_landed(nc * cs)
 
     total = jnp.sum(landed[...], axis=0)
     kind = lax.broadcasted_iota(jnp.int32, total.shape, 0)
     out_ref[...] = jnp.where(kind == 0, total / variants, 10.0 / variants * total)
 
-    @pl.when(mid)
-    def _():
-        for j in range(owners):
-            @pl.when(y * owners + j != me)
-            def _():
-                part_copy(j).wait_send()
+    def parts_sent(count):
+        slot = part.at[pl.ds(0, count)]
+        remote(slot, slot, part_send, part_recv, me).wait_send()
+
+    @pl.when(in_group)
+    def _():
+        parts_sent(owners - 1)
+
+    @pl.when(mid & jnp.logical_not(in_group))
+    def _():
+        parts_sent(owners)
 
 
 def local(dosage, covars, phenotypes):
@@ -592,10 +602,10 @@
     halves = 2
     hw = variants // peers // halves
     blocks = gh // LANES
-    group = max(g for g in range(1, 8) if blocks % g == 0)
+    cut = -(-blocks // peers)
     dma = pltpu.SemaphoreType.DMA
     out = pl.pallas_call(
-        functools.partial(kernel, n, zs, ys, cs, lo, hi, own, group),
+        functools.partial(kernel, n, zs, ys, cs, lo, hi, own),
         out_shape=pltpu.VMEM((2, LANES), F32),
         in_specs=[pl.BlockSpec(memory_space=pl.ANY)] * 3,
         out_specs=pl.BlockSpec(memory_space=pltpu.VMEM),
@@ -603,22 +613,17 @@
             pltpu.VMEM((rows, variants), BF16),
             pltpu.VMEM((rows, covs), F32),
             pltpu.VMEM((rows, gh), F32),
-            dma((4 + halves,)),
-            pltpu.VMEM((zs, cs, ys, 8, LANES), F32),
-            pltpu.VMEM((zs, cs, ys, rows, gh), F32),
-            pltpu.VMEM((halves, zs, cs, ys, rows, hw), BF16),
+            dma((4 + halves,)), dma((7,)),
+            pltpu.VMEM((n, 8, LANES), F32),
+            pltpu.VMEM((zs * cs, ys, rows, gh), F32),
+            pltpu.VMEM((halves, zs * cs, ys, rows, hw), BF16),
             pltpu.VMEM((halves, samples, hw), BF16),
             pltpu.VMEM((halves, 1, hw), F32),
             pltpu.VMEM((gh + LANES, samples), BF16),
             pltpu.VMEM((2, gh, LANES), F32),
             pltpu.VMEM((owners, 2, LANES), F32),
             pltpu.VMEM((peers, 2, LANES), F32),
-            dma((n,)), dma((n,)), dma, dma,
-            dma((hi - lo, cs, ys)), dma((ys,)), dma((zs, ys)),
-            dma((blocks, hi - lo)), dma((blocks,)), dma((blocks,)), dma((blocks,)), dma((blocks,)),
-            dma((halves, hi - lo, cs)), dma((halves, cs)), dma((halves, zs)),
-            dma((halves, zs)), dma((halves, zs)),
-            dma((owners,)), dma((peers,)),
+            dma((4,)), dma((hi - lo, 3, cut)), dma((halves, zs)), dma((halves,)),
         ],
         compiler_params=pltpu.CompilerParams(collective_id=0, has_side_effects=True),
     )(dosage, covars, phenotypes)

time: 29.3 us -> 28.3 us (0.966)
  Pallas kernels: 27.9 us -> 26.9 us
    pallas_call x1, Pallas kernels: 27.9 us -> 26.9 us  [local(): pl.pallas_call(functools.partial(kernel, n, zs, ys, cs, lo, hi, own), out...]
where the time goes in v3:
time: 28.3 us; the launch traced here: 28.1 us
  Pallas kernels  26.9 us (95%)
  between operations  0.64 us (2%)
  local copies, waits for them, and re-layouts  0.52 us (2%)
    pallas_call x1, Pallas kernels, local(): pl.pallas_call(functools.partial(kernel, n, zs, ys, cs, lo, hi, own), out...  26.9 us

profile of v3, /device:TPU:0, one launch (start us, length us, event | category | flops | bytes accessed | tf_op | source)
XLA Modules:
  0.0 28.1 jit_solution(11649203645562348995)
XLA Ops:
  0.6 26.9 %shard_map.50 = f32[2,128]{1,0:T(2,128)S(1)} custom-call(bf16[16,8192]{1,0:T(8,128)(2,1)} %dose_in.1, f32[16,16]{1,0:T(8,128)} %cov_in.1, f32[16,1792]{1,0:T(8,128)} %pheno_in.1), custom_call_target="tpu_custom_call" | custom-call | tf_op jit(solution)/shard_map/pallas_call | solution.py:607
  27.5 0.5 %slice_bitcast_fusion = (f32[112]{0:T(128)}, f32[112]{0:T(128)}) fusion(f32[2,128]{1,0:T(2,128)S(1)} %shard_map.50), kind=kLoop, calls=%fused_computation | loop fusion | bytes 1792 | tf_op jit(solution)/shard_map/squeeze | solution.py:630

commit v4 on v3

--- a/solution.py
+++ b/solution.py
@@ -57,18 +57,31 @@
 
 def scan(
     c, y, z, oc, other_row, cs, ys, zs, n, owners, me, place, own, halves, hw, samples, covs,
-    blocks, cut, cov_all, raw, dose_all, dres, vscale, pt, acc, part, landed, hand_on, cov_wait,
-    pheno_wait, resid_to, resid_pass, resid_wait, blocks_here, blocks_over, across_wait, d_recv,
-    remote, send_part, in_group, lane_slice,
+    blocks, cut, cov_all, raw, dose_all, dres, vscale, pt, acc, part, landed, hand_on, cov_wait, cov_over,
+    pheno_wait, pass_residuals, wait_residuals, across_wait, d_recv, remote, send_part,
+    in_group, lane_slice,
 ):
     far = range(2, zs)
     hand_on(0, [1])
 
-    cov_wait(n - 1)
-    tiles = cov_all[...]
+    cov_wait(n // cs - 1)
+    if cs > 1:
+        cov_over(c).start()
+    hand_on(0, far)
+    hand_on(1, [1])
+    if cs > 1:
+        cov_over(oc).wait_recv()
+    tiles = [
+        cov_all[ci, p * ys + yi] for p in range(zs) for ci in range(cs) for yi in range(ys)
+    ]
     cov = jnp.concatenate(
-        [tiles[:, :, i * covs : (i + 1) * covs] for i in range(samples // n // 8)], axis=1
-    ).reshape(samples, covs)
+        [
+            tile[:, i * covs : (i + 1) * covs]
+            for tile in tiles
+            for i in range(samples // n // 8)
+        ],
+        axis=0,
+    )
     covt = cov.T
     factor = inverse_factor(dot(covt, cov, 1, 0, HIGH))
     basist = dot(factor, covt, 1, 0, HIGH)
@@ -123,42 +136,30 @@
         pt[lane_slice(to * LANES, LANES), :] = (resid * lax.rsqrt(var)).astype(BF16).T
 
     def residuals():
-        for i in range(cut):
-            b = place * cut + i
-            residual(jnp.minimum(b, blocks - 1), jnp.minimum(b, blocks))
-        for i in range(cut):
-            resid_to(i)
-
-    def pass_residuals():
-        def body(b):
-            resid_wait(b).wait_recv()
-            if cs > 1:
-                resid_pass(b).start()
-
-        blocks_here(body)
-
-    def wait_residuals(own_plane):
-        if cs > 1:
-            blocks_over(lambda b: resid_pass(b).wait_recv(), own_plane)
-
-    mine = cs * cut
-    soon = blocks - (blocks - 1) // mine * mine
-
-    def associate(h, start, stop):
+        step = max(g for g in range(1, 8) if cut % g == 0)
+
+        @pl.loop(0, cut // step)
+        def _(i):
+            for g in range(step):
+                b = c * cut + i * step + g
+                residual(jnp.minimum(b, blocks - 1), jnp.minimum(b, blocks))
+
+        pass_residuals()
+
+    step = max(g for g in range(1, 8) if blocks % g == 0)
+
+    def associate(h):
         wide = min(2 * CHUNK, hw)
-        count = stop - start
-        step = max(g for g in range(1, 8) if count % g == 0)
 
         @pl.loop(0, hw // wide)
         def _(j):
             cols = lane_slice(j * wide, wide)
             scale = vscale[h, :, cols]
 
-            @pl.loop(0, count // step)
+            @pl.loop(0, blocks // step)
             def _(i):
                 for g in range(step):
-                    b = lax.rem(place // cs * mine + start + i * step + g, blocks)
-                    at = lane_slice(b * LANES, LANES)
+                    at = lane_slice((i * step + g) * LANES, LANES)
                     cross = dot(pt[at, :], dres[h, :, cols], 1, 0)
                     chi = cross * cross * scale
                     hit = 1.0 + jnp.tanh(chi - 4.0)
@@ -166,22 +167,14 @@
                     acc[1, at, :] += sum(hit[:, i : i + LANES] for i in range(0, wide, LANES))
 
     acc[...] = jnp.zeros_like(acc)
-    for h in range(1, halves):
-        hand_on(h, [1])
-    pheno_wait(zs * cs - 1)
+    hand_on(1, far)
+    dose_residuals(0)
+    pheno_wait()
     residuals()
-    for h in range(halves):
-        hand_on(h, far)
-    dose_residuals(0)
-    wait_residuals(True)
-    associate(0, 0, soon)
-    pass_residuals()
-    for h in range(1, halves):
-        dose_residuals(h)
-        associate(h, 0, soon)
-    wait_residuals(False)
-    for h in range(halves):
-        associate(h, soon, blocks)
+    dose_residuals(1)
+    wait_residuals()
+    associate(0)
+    associate(1)
 
     line = lax.broadcasted_iota(jnp.int32, (8, 4 * LANES), 0)
     lane = lax.broadcasted_iota(jnp.int32, (8, 4 * LANES), 1)
@@ -211,7 +204,7 @@
     n, zs, ys, cs, lo, hi, own,
     dose_in, cov_in, pheno_in, out_ref,
     dose_ref, cov_ref, pheno_ref, load_sem, sends, cov_all, raw, dose_all, dres, vscale, pt, acc,
-    part, landed, recvs, x_sem, d_recv, p_recv,
+    part, landed, recvs, heard, d_recv, p_recv,
 ):
     me = lax.axis_index("tile")
     rows, variants = dose_in.shape
@@ -231,8 +224,12 @@
     place = (z - lo) * cs + c
     own_row = z * cs + c
     other_row = z * cs + oc
-    cov_send, b_send, a_send, d_send, pass_send, part_send, xc_send = [sends.at[i] for i in range(7)]
-    cov_recv, b_recv, a_recv, part_recv = [recvs.at[i] for i in range(4)]
+    cov_send, b_send, a_send, over_send, d_send, pass_send, part_send, x_send, k_send = [
+        sends.at[i] for i in range(9)
+    ]
+    cov_recv, b_recv, a_recv, part_recv, x_recv, k_recv = [
+        recvs.at[i] for i in range(6)
+    ]
     mid = (z >= lo) & (z < hi)
     far = (2 * z) // zs
 
@@ -275,36 +272,70 @@
 
     barrier = pltpu.get_barrier_semaphore()
 
-    def greet(dev):
+    def tell(sem, dev):
         pl.semaphore_signal(
-            barrier, inc=1, device_id={"tile": dev}, device_id_type=pl.DeviceIdType.MESH
+            sem, inc=1, device_id={"tile": dev}, device_id_type=pl.DeviceIdType.MESH
         )
 
-    @pl.when(mid)
-    def _():
-        for k in range(1, n):
-            greet(lax.rem(me + k, n))
-
-    if ys > 1:
-        @pl.when(jnp.logical_not(mid))
-        def _():
-            greet(index(z, oy, c))
+    def tell_plane(sem):
+        for dy in range(ys):
+            for dc in range(cs):
+                if dy or dc:
+                    tell(sem, index(z, lax.rem(y + dy, ys), lax.rem(c + dc, cs)))
+
+    tell_plane(barrier)
+
+    @pl.when(z > 0)
+    def _():
+        tell(barrier, index(z - 1, y, c))
+
+    @pl.when(z + 1 < zs)
+    def _():
+        tell(barrier, index(z + 1, y, c))
 
     for load in loads:
         load.wait()
     packed = [cov_ref[g : g + 8, :] for g in range(0, rows, 8)]
     fill = jnp.zeros((8, LANES - len(packed) * covs), F32)
-    cov_all[own_row * ys + y] = jnp.concatenate(packed + [fill], axis=1)
+    cov_all[c, z * ys + y] = jnp.concatenate(packed + [fill], axis=1)
 
     @pl.when(mid)
     def _():
         for h in range(halves):
             own_dose(h).wait()
-        pl.semaphore_wait(barrier, nc * ys * cs - 1)
-
-    @pl.when(jnp.logical_not(mid))
-    def _():
-        pl.semaphore_wait(barrier, nc * ys * cs + (1 if ys > 1 else 0))
+
+    if zs > 1:
+        @pl.when((z > 0) & (z + 1 < zs))
+        def _():
+            pl.semaphore_wait(barrier, ys * cs + 1)
+
+        @pl.when((z == 0) | (z + 1 == zs))
+        def _():
+            pl.semaphore_wait(barrier, ys * cs)
+    elif ys * cs > 1:
+        pl.semaphore_wait(barrier, ys * cs - 1)
+    tell_plane(heard.at[0])
+
+    def hear_plane():
+        if ys * cs > 1:
+            pl.semaphore_wait(heard.at[0], ys * cs - 1)
+
+    def hear_all():
+        @pl.when(z + 1 < hi - 1)
+        def _():
+            pl.semaphore_wait(heard.at[1], 1)
+
+        @pl.when(z - 1 > lo)
+        def _():
+            pl.semaphore_wait(heard.at[2], 1)
+
+        @pl.when((z < hi - 1) & (z > 0))
+        def _():
+            tell(heard.at[1], index(z - 1, y, c))
+
+        @pl.when((z > lo) & (z + 1 < zs))
+        def _():
+            tell(heard.at[2], index(z + 1, y, c))
 
     def plane(i, body):
         p = jnp.where(mid, lo + lax.rem(z - lo + 1 + i + nc, nc), lo + i + far * (nc - 1 - 2 * i))
@@ -318,129 +349,97 @@
             plane(i, body)
 
     def cov_copies():
-        own_cov = cov_all.at[own_row * ys + y]
-        for j in range(nc * ys * cs):
-            dev = lo * ys * cs + j
+        own_cov = cov_all.at[c, z * ys + y]
+        for j in range(nc * ys):
+            dev = (lo * ys + j) * cs + c
 
             @pl.when(dev != me)
             def _():
                 remote(own_cov, own_cov, cov_send, cov_recv, dev).start()
 
     def cov_wait(count, send=False):
-        slot = cov_all.at[pl.ds(0, count)]
+        slot = cov_all.at[0, pl.ds(0, count)]
         copy = remote(slot, slot, cov_send, cov_recv, me)
         if send:
             copy.wait_send()
         else:
             copy.wait_recv()
 
+    def cov_over(ci):
+        slot = cov_all.at[ci]
+        return remote(slot, slot, k_send, k_recv, index(z, y, oc))
+
     def across():
         return remote(pheno_ref, raw.at[own_row, y], b_send, b_recv, index(z, oy, c))
 
     blocks = gh // LANES
-    cut = -(-blocks // (nc * cs))
-
-    def first(q):
-        return jnp.minimum(q * cut, blocks - cut)
-
-    def raw_slot(d, q):
-        lanes = lane_slice(first(q) * LANES, cut * LANES)
-        return raw.at[own_row, lax.rem(y + d, ys), :, lanes]
+    cut = -(-blocks // cs)
+
+    def genes_of(ci):
+        start = min(ci * cut, blocks)
+        return pl.ds(start * LANES, min(cut, blocks - start) * LANES)
+
+    def by_core(body):
+        for ci in range(cs):
+            @pl.when(c == ci)
+            def _():
+                body(ci)
 
     def pheno_to(d):
         def to(p):
             for ci in range(cs):
-                slot = raw_slot(d, (p - lo) * cs + ci)
+                slot = raw.at[own_row, lax.rem(y + d, ys), :, genes_of(ci)]
                 remote(slot, slot, a_send, a_recv, index(p, y, ci)).start()
 
         return to
 
     def pheno_over(d):
+        def body(ci):
+            slot = raw.at[own_row, lax.rem(y + d, ys), :, genes_of((ci + 1) % cs)]
+            remote(slot, slot, over_send, a_recv, index(z, y, oc)).start()
+
         if cs > 1:
             @pl.when(mid)
             def _():
-                slot = raw_slot(d, (z - lo) * cs + oc)
-                remote(slot, slot, a_send, a_recv, index(z, y, oc)).start()
-
-    def pheno_wait(count, send=False):
-        slot = raw.at[pl.ds(0, count), :, :, pl.ds(0, cut * LANES)]
-        copy = remote(slot, slot, a_send, a_recv, me)
-        if send:
-            copy.wait_send()
-        else:
-            copy.wait_recv()
-
-    def resid_slot(b):
-        return pt.at[pl.ds(pl.multiple_of(b * LANES, LANES), LANES)]
-
-    def resid_to(i):
-        b = place * cut + i
-
-        @pl.when(b < blocks)
-        def _():
-            for j in range(1, nc):
-                p = lo + lax.rem(z - lo + j, nc)
-                remote(
-                    resid_slot(b), resid_slot(b), x_sem.at[0, 0, i], x_sem.at[z - lo, 1, i],
-                    index(p, y, c),
-                ).start()
-            if cs > 1:
-                remote(
-                    resid_slot(b), resid_slot(b), x_sem.at[0, 0, i], x_sem.at[z - lo, 2, i],
-                    index(z, y, oc),
-                ).start()
-
-    def resid_sent(i):
-        slot = pt.at[pl.ds(0, (nc - 1 + (1 if cs > 1 else 0)) * LANES)]
-
-        @pl.when(place * cut + i < blocks)
-        def _():
-            remote(slot, slot, x_sem.at[0, 0, i], x_sem.at[0, 1, i], me).wait_send()
-
-    def resid_pass(b):
-        source = b // cut // cs
-        return remote(
-            resid_slot(b), resid_slot(b), xc_send, x_sem.at[source, 2, b % cut], index(z, y, oc)
-        )
-
-    def resid_wait(b):
-        source = b // cut // cs
-        return remote(resid_slot(b), resid_slot(b), xc_send, x_sem.at[source, 1, b % cut], me)
-
-    def blocks_here(body):
-        for b in range(blocks):
-            q = b // cut
-
-            @pl.when((c == q % cs) & (z != lo + q // cs))
-            def _():
-                body(b)
-
-    def blocks_over(body, own_plane):
-        for b in range(blocks):
-            q = b // cut
-            near = z == lo + q // cs
-
-            @pl.when((c != q % cs) & (near if own_plane else jnp.logical_not(near)))
-            def _():
-                body(b)
-
-    def passed_all():
-        for at in range(nc):
-            for ci in range(cs):
-                count = sum(b // cut % cs == ci and b // cut // cs != at for b in range(blocks))
-                if count:
-                    slot = pt.at[pl.ds(0, count * LANES)]
-
-                    @pl.when((z == lo + at) & (c == ci))
-                    def _():
-                        remote(slot, slot, xc_send, xc_send, me).wait_send()
+                by_core(body)
+
+    def pheno_wait():
+        def body(ci):
+            slot = raw.at[pl.ds(0, zs * cs - 1), :, :, genes_of(ci)]
+            remote(slot, slot, a_send, a_recv, me).wait_recv()
+
+        by_core(body)
+
+    def pheno_sent(count):
+        slot = raw.at[pl.ds(0, count)]
+        remote(slot, slot, a_send, a_recv, me).wait_send()
+
+    def over_sent():
+        def body(ci):
+            slot = raw.at[0, :, :, genes_of((ci + 1) % cs)]
+            remote(slot, slot, over_send, a_recv, me).wait_send()
+
+        by_core(body)
+
+    def resid_copy(ci):
+        slot = pt.at[genes_of(ci)]
+        return remote(slot, slot, x_send, x_recv, index(z, y, oc))
+
+    def pass_residuals():
+        if cs > 1:
+            by_core(lambda ci: resid_copy(ci).start())
+
+    def wait_residuals():
+        if cs > 1:
+            by_core(lambda ci: resid_copy((ci + 1) % cs).wait_recv())
 
     def block(p, ci, h):
         return dose_ref.at[:, lane_slice(((p - lo) * cs + ci) * width + h * hw, hw)]
 
-    def dose_to(h):
+    def dose_to(h, cores=(0, 1)):
         def to(p):
-            for ci in range(cs):
+            for dc in cores[:cs]:
+                ci = lax.rem(c + dc, cs)
                 remote(
                     block(p, ci, h), dose_all.at[h, own_row, y], d_send, d_recv.at[h, z],
                     index(p, y, ci),
@@ -501,14 +500,28 @@
         for k in ks:
             at_distance(k, body)
 
+    next_door = nc == 2 and lo == 1
+    if not next_door:
+        hear_plane()
+        hear_all()
     if ys > 1:
         across().start()
     own_copies(0)
-    plane(0, dose_to(0))
+    plane(0, dose_to(0, (0,)))
+    own_copies(1)
+    plane(0, dose_to(1, (0,)))
+    if next_door:
+        hear_plane()
+        hear_all()
+    if cs > 1:
+        plane(0, dose_to(0, (1,)))
+    for i in range(1, nc):
+        plane(i, dose_to(0))
     cov_copies()
-    for h in range(1, halves):
-        own_copies(h)
-        plane(0, dose_to(h))
+    if cs > 1:
+        plane(0, dose_to(1, (1,)))
+    for i in range(1, nc):
+        plane(i, dose_to(1))
     pheno_over(0)
     for i in range(nc):
         plane(i, pheno_to(0))
@@ -518,9 +531,6 @@
         pheno_over(1)
         for i in range(nc):
             plane(i, pheno_to(1))
-    for i in range(1, nc):
-        for h in range(halves):
-            plane(i, dose_to(h))
 
     in_group = mid & (me // owners == y)
 
@@ -532,8 +542,8 @@
         scan(
             c, y, z, oc, other_row, cs, ys, zs, n, owners, me, place, own, halves, hw, samples,
             covs, blocks, cut, cov_all, raw, dose_all, dres, vscale, pt, acc, part, landed,
-            hand_on, cov_wait, pheno_wait, resid_to, resid_pass, resid_wait, blocks_here,
-            blocks_over, across_wait, d_recv, remote, send_part, in_group, lane_slice,
+            hand_on, cov_wait, cov_over, pheno_wait, pass_residuals, wait_residuals, across_wait, d_recv,
+            remote, send_part, in_group, lane_slice,
         )
 
     if ys > 1:
@@ -541,19 +551,22 @@
 
     @pl.when(mid)
     def _():
-        cov_wait(nc * ys * cs - 1, send=True)
-        pheno_wait((nc - 1) * cs + (1 if cs > 1 else 0), send=True)
+        cov_wait(nc * ys - 1, send=True)
+        if cs > 1:
+            cov_over(c).wait_send()
+        if nc > 1:
+            pheno_sent(nc - 1)
+        if cs > 1:
+            over_sent()
+            by_core(lambda ci: resid_copy(ci).wait_send())
         dose_sent((nc - 1) * cs + (cs if ys > 1 else 0) + (1 if cs > 1 else 0))
         if ys > 1:
             passes_sent()
-        for i in range(cut):
-            resid_sent(i)
-        passed_all()
 
     @pl.when(jnp.logical_not(mid))
     def _():
-        cov_wait(nc * ys * cs, send=True)
-        pheno_wait(nc * cs, send=True)
+        cov_wait(nc * ys, send=True)
+        pheno_sent(nc)
         dose_sent(nc * cs)
 
     def parts_landed(count):
@@ -602,7 +615,6 @@
     halves = 2
     hw = variants // peers // halves
     blocks = gh // LANES
-    cut = -(-blocks // peers)
     dma = pltpu.SemaphoreType.DMA
     out = pl.pallas_call(
         functools.partial(kernel, n, zs, ys, cs, lo, hi, own),
@@ -613,8 +625,8 @@
             pltpu.VMEM((rows, variants), BF16),
             pltpu.VMEM((rows, covs), F32),
             pltpu.VMEM((rows, gh), F32),
-            dma((4 + halves,)), dma((7,)),
-            pltpu.VMEM((n, 8, LANES), F32),
+            dma((4 + halves,)), dma((9,)),
+            pltpu.VMEM((cs, n // cs, 8, LANES), F32),
             pltpu.VMEM((zs * cs, ys, rows, gh), F32),
             pltpu.VMEM((halves, zs * cs, ys, rows, hw), BF16),
             pltpu.VMEM((halves, samples, hw), BF16),
@@ -623,7 +635,7 @@
             pltpu.VMEM((2, gh, LANES), F32),
             pltpu.VMEM((owners, 2, LANES), F32),
             pltpu.VMEM((peers, 2, LANES), F32),
-            dma((4,)), dma((hi - lo, 3, cut)), dma((halves, zs)), dma((halves,)),
+            dma((6,)), pltpu.SemaphoreType.REGULAR((3,)), dma((halves, zs)), dma((halves,)),
         ],
         compiler_params=pltpu.CompilerParams(collective_id=0, has_side_effects=True),
     )(dosage, covars, phenotypes)

time: 28.3 us -> 27.4 us (0.968)
  Pallas kernels: 26.9 us -> 26.1 us
    pallas_call x1, Pallas kernels: 26.9 us -> 26.1 us  [local(): pl.pallas_call(functools.partial(kernel, n, zs, ys, cs, lo, hi, own), out...]
where the time goes in v4:
time: 27.4 us; the launch traced here: 27.2 us
  Pallas kernels  26.1 us (95%)
  between operations  0.64 us (2%)
  local copies, waits for them, and re-layouts  0.52 us (2%)
    pallas_call x1, Pallas kernels, local(): pl.pallas_call(functools.partial(kernel, n, zs, ys, cs, lo, hi, own), out...  26.1 us

profile of v4, /device:TPU:0, one launch (start us, length us, event | category | flops | bytes accessed | tf_op | source)
XLA Modules:
  0.0 27.2 jit_solution(4719097166789656156)
XLA Ops:
  0.6 26.1 %shard_map.50 = f32[2,128]{1,0:T(2,128)S(1)} custom-call(bf16[16,8192]{1,0:T(8,128)(2,1)} %dose_in.1, f32[16,16]{1,0:T(8,128)} %cov_in.1, f32[16,1792]{1,0:T(8,128)} %pheno_in.1), custom_call_target="tpu_custom_call" | custom-call | tf_op jit(solution)/shard_map/pallas_call | solution.py:619
  26.7 0.5 %slice_bitcast_fusion = (f32[112]{0:T(128)}, f32[112]{0:T(128)}) fusion(f32[2,128]{1,0:T(2,128)S(1)} %shard_map.50), kind=kLoop, calls=%fused_computation | loop fusion | bytes 1792 | tf_op jit(solution)/shard_map/squeeze | solution.py:642

commit v5 on v4

--- a/solution.py
+++ b/solution.py
@@ -146,25 +146,40 @@
 
         pass_residuals()
 
-    step = max(g for g in range(1, 8) if blocks % g == 0)
-
-    def associate(h):
-        wide = min(2 * CHUNK, hw)
+    def associate(h, start, stop):
+        wide = hw
+        count = stop - start
+        step = max(g for g in range(1, 8) if count % g == 0)
 
         @pl.loop(0, hw // wide)
         def _(j):
             cols = lane_slice(j * wide, wide)
             scale = vscale[h, :, cols]
 
-            @pl.loop(0, blocks // step)
+            @pl.loop(0, count // step)
             def _(i):
                 for g in range(step):
-                    at = lane_slice((i * step + g) * LANES, LANES)
+                    at = lane_slice((start + i * step + g) * LANES, LANES)
                     cross = dot(pt[at, :], dres[h, :, cols], 1, 0)
                     chi = cross * cross * scale
                     hit = 1.0 + jnp.tanh(chi - 4.0)
                     acc[0, at, :] += sum(chi[:, i : i + LANES] for i in range(0, wide, LANES))
                     acc[1, at, :] += sum(hit[:, i : i + LANES] for i in range(0, wide, LANES))
+
+    line = lax.broadcasted_iota(jnp.int32, (8, 4 * LANES), 0)
+    lane = lax.broadcasted_iota(jnp.int32, (8, 4 * LANES), 1)
+    pick = (lane // (2 * LANES) == line).astype(F32).astype(BF16)
+
+    def parts(start, stop):
+        for j in range(start, stop):
+            at = pl.ds(j * own, own)
+            terms = split(acc[0, at, :], 2) + split(acc[1, at, :], 2)
+            sums = dot(pick, jnp.concatenate(terms, axis=1), 1, 1)
+            part[j, :, pl.ds(0, own)] = sums[0:2, :]
+        for j in range(start, stop):
+            @pl.when(y * owners + j != me)
+            def _():
+                send_part(j)
 
     acc[...] = jnp.zeros_like(acc)
     hand_on(1, far)
@@ -173,27 +188,13 @@
     residuals()
     dose_residuals(1)
     wait_residuals()
-    associate(0)
-    associate(1)
-
-    line = lax.broadcasted_iota(jnp.int32, (8, 4 * LANES), 0)
-    lane = lax.broadcasted_iota(jnp.int32, (8, 4 * LANES), 1)
-    pick = (lane // (2 * LANES) == line).astype(F32).astype(BF16)
-
-    @pl.loop(0, owners // 8)
-    def _(b):
-        for i in range(8):
-            j = b * 8 + i
-            at = pl.ds(pl.multiple_of(j * own, 8), own)
-            terms = split(acc[0, at, :], 2) + split(acc[1, at, :], 2)
-            sums = dot(pick, jnp.concatenate(terms, axis=1), 1, 1)
-            part[j, :, pl.ds(0, own)] = sums[0:2, :]
-        for i in range(8):
-            j = b * 8 + i
-
-            @pl.when(y * owners + j != me)
-            def _():
-                send_part(j)
+    at = owner = 0
+    for stop in (-(-blocks * 2 // 7), -(-blocks * 4 // 7), blocks):
+        for h in range(halves):
+            associate(h, at, stop)
+        ready = stop * LANES // own if stop < blocks else owners
+        parts(owner, ready)
+        at, owner = stop, ready
 
     @pl.when(in_group)
     def _():

time: 27.4 us -> 25.5 us (0.931)
  Pallas kernels: 26.1 us -> 24 us
    pallas_call x1, Pallas kernels: 26.1 us -> 24 us  [local(): pl.pallas_call(functools.partial(kernel, n, zs, ys, cs, lo, hi, own), out...]
where the time goes in v5:
time: 25.5 us; the launch traced here: 25.1 us
  Pallas kernels  24 us (94%)
  between operations  0.64 us (3%)
  local copies, waits for them, and re-layouts  0.52 us (2%)
    pallas_call x1, Pallas kernels, local(): pl.pallas_call(functools.partial(kernel, n, zs, ys, cs, lo, hi, own), out...  24 us
    squeeze x1, local copies, waits for them, and re-layouts, local(): return (out[0, :own], out[1, :own])  0.52 us

profile of v5, /device:TPU:0, one launch (start us, length us, event | category | flops | bytes accessed | tf_op | source)
XLA Modules:
  0.0 25.1 jit_solution(2253719795417570553)
XLA Ops:
  0.6 24.0 %shard_map.50 = f32[2,128]{1,0:T(2,128)S(1)} custom-call(bf16[16,8192]{1,0:T(8,128)(2,1)} %dose_in.1, f32[16,16]{1,0:T(8,128)} %cov_in.1, f32[16,1792]{1,0:T(8,128)} %pheno_in.1), custom_call_target="tpu_custom_call" | custom-call | tf_op jit(solution)/shard_map/pallas_call | solution.py:620
  24.6 0.5 %slice_bitcast_fusion = (f32[112]{0:T(128)}, f32[112]{0:T(128)}) fusion(f32[2,128]{1,0:T(2,128)S(1)} %shard_map.50), kind=kLoop, calls=%fused_computation | loop fusion | bytes 1792 | tf_op jit(solution)/shard_map/squeeze | solution.py:643

commit v6 on v5

--- a/solution.py
+++ b/solution.py
@@ -120,9 +120,11 @@
         for j in range(hw // CHUNK):
             dose_residual(h, j)
 
-    def residual(b, to):
-        at = b * LANES
-        pheno = raw[:, :, :, lane_slice(at, LANES)].reshape(samples, LANES)
+    wide = max(g for g in range(1, 5) if cut % g == 0)
+
+    def residual(b):
+        genes = raw[:, :, :, lane_slice(b * LANES, wide * LANES)]
+        pheno = genes.reshape(samples, wide * LANES)
         hi, mid, low = split(pheno, 3)
         with_hi = dot(bt, hi, 1, 0)
         with_mid = dot(bt[0 : 2 * covs], mid, 1, 0)
@@ -133,38 +135,41 @@
         )
         resid = pheno - fitted(coef)
         var = jnp.sum(resid * resid, axis=0, keepdims=True) / samples + 0.1
-        pt[lane_slice(to * LANES, LANES), :] = (resid * lax.rsqrt(var)).astype(BF16).T
+        resid = (resid * lax.rsqrt(var)).astype(BF16).T
+        for g in range(wide):
+            to = jnp.where((b + g) // cut == c, b + g, blocks)
+            pt[lane_slice(to * LANES, LANES), :] = resid[g * LANES : (g + 1) * LANES]
 
     def residuals():
-        step = max(g for g in range(1, 8) if cut % g == 0)
-
-        @pl.loop(0, cut // step)
+        @pl.loop(0, cut // wide)
         def _(i):
+            residual(jnp.minimum(c * cut + i * wide, blocks - wide))
+
+        pass_residuals()
+
+    def associate(start, stop):
+        count = stop - start
+        step = max(g for g in range(1, 5) if count % g == 0)
+
+        def group(first):
             for g in range(step):
-                b = c * cut + i * step + g
-                residual(jnp.minimum(b, blocks - 1), jnp.minimum(b, blocks))
-
-        pass_residuals()
-
-    def associate(h, start, stop):
-        wide = hw
-        count = stop - start
-        step = max(g for g in range(1, 8) if count % g == 0)
-
-        @pl.loop(0, hw // wide)
-        def _(j):
-            cols = lane_slice(j * wide, wide)
-            scale = vscale[h, :, cols]
-
+                at = lane_slice((first + g) * LANES, LANES)
+                chis, hits = [], []
+                for h in range(halves):
+                    cross = dot(pt[at, :], dres[h], 1, 0)
+                    chi = cross * cross * vscale[h]
+                    hit = 1.0 + jnp.tanh(chi - 4.0)
+                    chis += [chi[:, i : i + LANES] for i in range(0, hw, LANES)]
+                    hits += [hit[:, i : i + LANES] for i in range(0, hw, LANES)]
+                acc[0, at, :] = sum(chis)
+                acc[1, at, :] = sum(hits)
+
+        if count == step:
+            group(start)
+        else:
             @pl.loop(0, count // step)
             def _(i):
-                for g in range(step):
-                    at = lane_slice((start + i * step + g) * LANES, LANES)
-                    cross = dot(pt[at, :], dres[h, :, cols], 1, 0)
-                    chi = cross * cross * scale
-                    hit = 1.0 + jnp.tanh(chi - 4.0)
-                    acc[0, at, :] += sum(chi[:, i : i + LANES] for i in range(0, wide, LANES))
-                    acc[1, at, :] += sum(hit[:, i : i + LANES] for i in range(0, wide, LANES))
+                group(start + i * step)
 
     line = lax.broadcasted_iota(jnp.int32, (8, 4 * LANES), 0)
     lane = lax.broadcasted_iota(jnp.int32, (8, 4 * LANES), 1)
@@ -181,7 +186,6 @@
             def _():
                 send_part(j)
 
-    acc[...] = jnp.zeros_like(acc)
     hand_on(1, far)
     dose_residuals(0)
     pheno_wait()
@@ -190,8 +194,7 @@
     wait_residuals()
     at = owner = 0
     for stop in (-(-blocks * 2 // 7), -(-blocks * 4 // 7), blocks):
-        for h in range(halves):
-            associate(h, at, stop)
+        associate(at, stop)
         ready = stop * LANES // own if stop < blocks else owners
         parts(owner, ready)
         at, owner = stop, ready
@@ -288,11 +291,13 @@
 
     @pl.when(z > 0)
     def _():
-        tell(barrier, index(z - 1, y, c))
+        for ci in range(cs):
+            tell(barrier, index(z - 1, y, ci))
 
     @pl.when(z + 1 < zs)
     def _():
-        tell(barrier, index(z + 1, y, c))
+        for ci in range(cs):
+            tell(barrier, index(z + 1, y, ci))
 
     for load in loads:
         load.wait()
@@ -308,11 +313,11 @@
     if zs > 1:
         @pl.when((z > 0) & (z + 1 < zs))
         def _():
-            pl.semaphore_wait(barrier, ys * cs + 1)
+            pl.semaphore_wait(barrier, ys * cs - 1 + 2 * cs)
 
         @pl.when((z == 0) | (z + 1 == zs))
         def _():
-            pl.semaphore_wait(barrier, ys * cs)
+            pl.semaphore_wait(barrier, ys * cs - 1 + cs)
     elif ys * cs > 1:
         pl.semaphore_wait(barrier, ys * cs - 1)
     tell_plane(heard.at[0])
@@ -508,23 +513,20 @@
     if ys > 1:
         across().start()
     own_copies(0)
-    plane(0, dose_to(0, (0,)))
+    plane(0, dose_to(0))
     own_copies(1)
-    plane(0, dose_to(1, (0,)))
+    pheno_over(0)
+    plane(0, pheno_to(0))
     if next_door:
         hear_plane()
         hear_all()
-    if cs > 1:
-        plane(0, dose_to(0, (1,)))
     for i in range(1, nc):
         plane(i, dose_to(0))
     cov_copies()
-    if cs > 1:
-        plane(0, dose_to(1, (1,)))
+    plane(0, dose_to(1))
     for i in range(1, nc):
         plane(i, dose_to(1))
-    pheno_over(0)
-    for i in range(nc):
+    for i in range(1, nc):
         plane(i, pheno_to(0))
     if ys > 1:
         slot = raw.at[own_row, oy]

time: 25.5 us -> 25.3 us (level)
  Pallas kernels: 24 us -> 23.7 us
    pallas_call x1, Pallas kernels: 24 us -> 23.7 us  [local(): pl.pallas_call(functools.partial(kernel, n, zs, ys, cs, lo, hi, own), out...]
where the time goes in v6:
time: 25.3 us; the launch traced here: 24.8 us
  Pallas kernels  23.7 us (94%)
  between operations  0.64 us (3%)
  local copies, waits for them, and re-layouts  0.52 us (2%)
    pallas_call x1, Pallas kernels, local(): pl.pallas_call(functools.partial(kernel, n, zs, ys, cs, lo, hi, own), out...  23.7 us
    squeeze x1, local copies, waits for them, and re-layouts, local(): return (out[0, :own], out[1, :own])  0.52 us

profile of v6, /device:TPU:0, one launch (start us, length us, event | category | flops | bytes accessed | tf_op | source)
XLA Modules:
  0.0 24.8 jit_solution(10884583830365884858)
XLA Ops:
  0.6 23.7 %shard_map.50 = f32[2,128]{1,0:T(2,128)S(1)} custom-call(bf16[16,8192]{1,0:T(8,128)(2,1)} %dose_in.1, f32[16,16]{1,0:T(8,128)} %cov_in.1, f32[16,1792]{1,0:T(8,128)} %pheno_in.1), custom_call_target="tpu_custom_call" | custom-call | tf_op jit(solution)/shard_map/pallas_call | solution.py:622
  24.3 0.5 %slice_bitcast_fusion = (f32[112]{0:T(128)}, f32[112]{0:T(128)}) fusion(f32[2,128]{1,0:T(2,128)S(1)} %shard_map.50), kind=kLoop, calls=%fused_computation | loop fusion | bytes 1792 | tf_op jit(solution)/shard_map/squeeze | solution.py:645
